TPU v7x, 256 devices: a whole 4x4x8 slice. The times are simulated.
256 devices in a mesh: comm: 8 (over z), arc: 32 (over y, x, core).
Axes of the slice: x: 4, y: 4, z: 8, core: 2. Of those that a mesh axis runs over, the one named last changes fastest.
Arguments:
- prev_dist: float32 [1024, 8192], P('comm', 'arc'), may hold values from 0 to 4
- source_node: int32 [1024], P('comm'), may hold values from 0 to 8191, as said below
- arc_tail: int32 [16, 8192], P(None, 'arc'), may hold values from 0 to 8191, as said below
- base_cost: float32 [16, 8192], P(None, 'arc'), may hold values from 0.05 to 1
- arc_price: float32 [16, 8192], P(None, 'arc'), may hold values from 0 to 1
- capacity: float32 [16, 8192], P(None, 'arc')
- path_arcs: int32 [1024, 128], P(('comm', 'arc')), may hold values from 0 to 131071, as said below
- demand: float32 [1024], P(('comm', 'arc')), may hold values from 0.5 to 2
Outputs:
- final_dist: float32 [1024, 8192], P('comm', 'arc')
- new_price: float32 [16, 8192], P(None, 'arc')
Inputs may be any that keep to these rules, and one draw needn't show every extreme that they name: `arc_tail`: the tail of arc s * 8192 + v lies in a node block (nodes 128 b to 128 b + 127) at most 2 blocks before or after v's block, counted around the cycle of blocks. Row k is a walk: the head of path_arcs[k, h + 1] (its id modulo 8192) is the tail of path_arcs[k, h]. `source_node`: the tail of path_arcs[k, 127].
All inputs are finite; a program needn't handle non-finite values.
Results may differ from a plain program's by a relative error of at most 0.00002.
Values sent between devices are 32-bit elements; how exact they have to be, the bound alone decides.
A program may use at most 64 MiB of HBM per device.

v0:
```python
import jax
import jax.numpy as jnp
from jax import lax
from jax.sharding import PartitionSpec as P

SWEEPS = 8


step_size = 0.25
eps_value = 1e-06


def with_halo(cells, sides, width):
    for axis, dim in sides:
        count = lax.axis_size(axis)
        head = lax.slice_in_dim(cells, 0, width, axis=dim)
        tail = lax.slice_in_dim(cells, cells.shape[dim] - width, cells.shape[dim], axis=dim)
        cells = jnp.concatenate(
            [
                lax.ppermute(tail, axis, [(i, (i + 1) % count) for i in range(count)]),
                cells,
                lax.ppermute(head, axis, [((i + 1) % count, i) for i in range(count)]),
            ],
            axis=dim,
        )
    return cells


def in_blocks(array, dim, size):
    lengths = array.shape
    tiles = array.reshape(*lengths[:dim], size, lengths[dim] // size, *lengths[dim + 1 :])
    return jnp.moveaxis(tiles, dim, 0)


def sent_and_summed(array, axis, dim):
    tiles = in_blocks(array, dim, lax.axis_size(axis))
    arrived = lax.all_to_all(tiles, axis, split_axis=0, concat_axis=0, tiled=True)
    return arrived.sum(axis=0)


def copy_for_each(array, axis):
    size = lax.axis_size(axis)
    return lax.all_to_all(
        jnp.broadcast_to(array[None], (size, *array.shape)), axis, 0, 0, tiled=True
    )


def taken_together(array, axis):
    everything = copy_for_each(array, axis)
    return jnp.sum(everything, axis=0)


def relax(window, window_start, tail_nodes, weights, current, node_count):
    degree = tail_nodes.shape[0]
    node_span = tail_nodes.shape[1]
    local_index = jnp.mod(tail_nodes - window_start, node_count).reshape(-1)
    picked = jnp.take(window, local_index, axis=0).reshape(degree, node_span, window.shape[1])
    candidate = picked + weights[:, :, None]
    return jnp.minimum(current, jnp.min(candidate, axis=0))


def shards(prev_dist, source_node, arc_tail, base_cost, arc_price, capacity, path_arcs, demand):
    shard_nodes = prev_dist.shape[1]
    arc_devices = lax.axis_size("arc")
    node_count = shard_nodes * arc_devices
    degree = arc_tail.shape[0]
    sweep_total = SWEEPS
    first_node = lax.axis_index("arc") * shard_nodes
    node_ids = first_node + jnp.arange(shard_nodes, dtype=jnp.int32)
    arc_weight = base_cost + arc_price
    node_major = jnp.where(node_ids[:, None] == source_node[None, :], jnp.float32(0.0), prev_dist.T)
    for sweep_number in range(sweep_total):
        window = with_halo(node_major, (("arc", 0),), shard_nodes)
        node_major = relax(
            window, first_node - shard_nodes, arc_tail, arc_weight, node_major, node_count
        )
    distance = node_major.T
    amounts = jnp.broadcast_to(demand[:, None], path_arcs.shape).reshape(-1)
    flattened = (
        jnp.zeros((degree * node_count,), jnp.float32).at[path_arcs.reshape(-1)].add(amounts)
    )
    partial_flow = sent_and_summed(flattened.reshape(degree, node_count), "arc", 1)
    arc_flow = taken_together(partial_flow, "comm")
    gradient = arc_flow - capacity
    square_sum = taken_together(jnp.sum(gradient * gradient), "arc")
    scale_root = jnp.sqrt(square_sum / (degree * node_count) + eps_value)
    new_price = jnp.maximum(arc_price + step_size * gradient / scale_root, jnp.float32(0.0))
    return (distance, new_price)


def solution(mesh):
    in_specs = (
        P("comm", "arc"),
        P("comm"),
        P(None, "arc"),
        P(None, "arc"),
        P(None, "arc"),
        P(None, "arc"),
        P(("comm", "arc"), None),
        P(("comm", "arc")),
    )
    out_specs = (P("comm", "arc"), P(None, "arc"))
    return jax.shard_map(shards, mesh=mesh, in_specs=in_specs, out_specs=out_specs, check_vma=False)
```

profile of v0, /device:TPU:32, one launch (start us, length us, event | category | flops | bytes accessed | tf_op | source)
XLA Modules:
  0.0 218.1 jit_solution(9169331098678607756)
XLA Ops:
  1.5 3.4 %scatter_custom_fusion = f32[131072]{0:T(1024)S(1)} fusion(s32[512]{0:T(512)S(1)} %bitcast.62, f32[512]{0:T(512)S(1)} %broadcast_bitcast_fusion, f32[]{:T(128)} %constant.60.clone.1), kind=kCustom, calls=%fused_computation.33 | custom fusion | flops 512 | bytes 524292 | tf_op jit(solution)/shard_map/scatter-add | solution.py:80
  6.1 7.3 %all-to-all-start = ((f32[32,16,256]{2,1,0:T(8,128)}), f32[32,16,256]{2,1,0:T(8,128)S(1)}, u32[]{:S(2)}, u32[]{:S(2)}) async-start(f32[32,16,256]{2,1,0:T(8,128)} %copy.26), calls=%async_computation | async-start | bytes 1048576 | tf_op jit(solution)/shard_map/all_to_all | solution.py:37
  13.7 5.0 %collective-permute-start.1 = (f32[256,128]{1,0:T(8,128)S(1)}, f32[256,128]{1,0:T(8,128)S(1)}, u32[]{:S(2)}, u32[]{:S(2)}) collective-permute-start(f32[256,128]{1,0:T(8,128)S(1)} %bitcast_select_fusion), channel_id=1, source_target_pairs={{1,0},{2,1},{3,2},{4,3},{5,4},{6,5},{7,6},{8,7},{9,8},{10,9},{11,1... | collective-permute-start | bytes 393224 | tf_op jit(solution)/shard_map/ppermute | solution.py:22
  18.7 6.3 %all-to-all-done = f32[32,16,256]{2,1,0:T(8,128)S(1)} async-done(((f32[32,16,256]{2,1,0:T(8,128)}), f32[32,16,256]{2,1,0:T(8,128)S(1)}, u32[]{:S(2)}, u32[]{:S(2)}) %all-to-all-start) | async-done | bytes 524320 | tf_op jit(solution)/shard_map/all_to_all | solution.py:37
  25.7 8.6 %all-to-all-start.1 = ((f32[8,16,256]{2,1,0:T(8,128)}), f32[8,16,256]{2,1,0:T(8,128)S(1)}, u32[]{:S(2)}, u32[]{:S(2)}) async-start(f32[8,16,256]{2,1,0:T(8,128)} %broadcast_in_dim.27), calls=%async_computation.1 | async-start | bytes 262144 | tf_op jit(solution)/shard_map/all_to_all | solution.py:43
  34.4 14.1 %gather_fusion = f32[4096,128]{1,0:T(8,128)} fusion(f32[768,128]{1,0:T(8,128)S(1)} %pad_maximum_fusion, s32[4096]{0:T(1024)S(1)} %fusion.4), kind=kCustom, calls=%fused_computation.clone | custom fusion | bytes 4210688 | tf_op jit(solution)/shard_map/jit(_take)/gather | solution.py:57
  50.4 4.1 %all-to-all-start.2 = ((f32[32,1,1]{2,1,0:T(1,128)}), f32[32,1,1]{2,1,0:T(1,128)S(1)}, u32[]{:S(2)}, u32[]{:S(2)}) async-start(f32[32,1,1]{2,1,0:T(1,128)} %broadcast_in_dim.28), calls=%async_computation.2 | async-start | bytes 32768 | tf_op jit(solution)/shard_map/all_to_all | solution.py:43
  54.5 3.6 %broadcast_select_fusion.7 = f32[4096,128]{1,0:T(8,128)S(1)} fusion(f32[4096,128]{1,0:T(8,128)} %gather_fusion, pred[4096]{0:T(1024)(128)(4,1)S(1)} %compare_and_fusion), kind=kLoop, calls=%fused_computation.24 | loop fusion | flops 524288 | bytes 4198400 | tf_op jit(solution)/shard_map/jit(_take)/select_n | solution.py:57
  58.1 3.7 %all-to-all-done.2 = f32[32,1,1]{2,1,0:T(1,128)S(1)} async-done(((f32[32,1,1]{2,1,0:T(1,128)}), f32[32,1,1]{2,1,0:T(1,128)S(1)}, u32[]{:S(2)}, u32[]{:S(2)}) %all-to-all-start.2) | async-done | bytes 160 | tf_op jit(solution)/shard_map/all_to_all | solution.py:43
  65.9 2.5 %collective-permute-done.3 = f32[256,128]{1,0:T(8,128)S(1)} collective-permute-done((f32[256,128]{1,0:T(8,128)S(1)}, f32[256,128]{1,0:T(8,128)S(1)}, u32[]{:S(2)}, u32[]{:S(2)}) %collective-permute-start.3) | collective-permute-done | bytes 131104 | tf_op jit(solution)/shard_map/ppermute | solution.py:22
  68.5 5.2 %collective-permute-done.2 = f32[256,128]{1,0:T(8,128)S(1)} collective-permute-done((f32[256,128]{1,0:T(8,128)S(1)}, f32[256,128]{1,0:T(8,128)S(1)}, u32[]{:S(2)}, u32[]{:S(2)}) %collective-permute-start.2) | collective-permute-done | bytes 131104 | tf_op jit(solution)/shard_map/ppermute | solution.py:20
  73.7 10.8 %gather_fusion.1 = f32[4096,128]{1,0:T(8,128)S(1)} fusion(f32[768,128]{1,0:T(8,128)S(1)} %pad_maximum_fusion.1, s32[4096]{0:T(1024)S(1)} %fusion.4), kind=kCustom, calls=%fused_computation.1.clone | custom fusion | bytes 4210688 | tf_op jit(solution)/shard_map/jit(_take)/gather | solution.py:57
  84.5 2.1 broadcast_select_fusion.6
  87.9 2.0 collective-permute-done.5
  90.0 5.3 %collective-permute-done.4 = f32[256,128]{1,0:T(8,128)S(1)} collective-permute-done((f32[256,128]{1,0:T(8,128)S(1)}, f32[256,128]{1,0:T(8,128)S(1)}, u32[]{:S(2)}, u32[]{:S(2)}) %collective-permute-start.4) | collective-permute-done | bytes 131104 | tf_op jit(solution)/shard_map/ppermute | solution.py:20
  95.3 10.8 %gather_fusion.2 = f32[4096,128]{1,0:T(8,128)S(1)} fusion(f32[768,128]{1,0:T(8,128)S(1)} %pad_maximum_fusion.2, s32[4096]{0:T(1024)S(1)} %fusion.4), kind=kCustom, calls=%fused_computation.2.clone | custom fusion | bytes 4210688 | tf_op jit(solution)/shard_map/jit(_take)/gather | solution.py:57
  106.1 2.1 broadcast_select_fusion.5
  111.7 5.3 %collective-permute-done.6 = f32[256,128]{1,0:T(8,128)S(1)} collective-permute-done((f32[256,128]{1,0:T(8,128)S(1)}, f32[256,128]{1,0:T(8,128)S(1)}, u32[]{:S(2)}, u32[]{:S(2)}) %collective-permute-start.6) | collective-permute-done | bytes 131104 | tf_op jit(solution)/shard_map/ppermute | solution.py:20
  117.0 10.8 %gather_fusion.3 = f32[4096,128]{1,0:T(8,128)S(1)} fusion(f32[768,128]{1,0:T(8,128)S(1)} %pad_maximum_fusion.3, s32[4096]{0:T(1024)S(1)} %fusion.4), kind=kCustom, calls=%fused_computation.3.clone | custom fusion | bytes 4210688 | tf_op jit(solution)/shard_map/jit(_take)/gather | solution.py:57
  127.8 2.1 broadcast_select_fusion.4
  133.3 5.3 %collective-permute-done.8 = f32[256,128]{1,0:T(8,128)S(1)} collective-permute-done((f32[256,128]{1,0:T(8,128)S(1)}, f32[256,128]{1,0:T(8,128)S(1)}, u32[]{:S(2)}, u32[]{:S(2)}) %collective-permute-start.8) | collective-permute-done | bytes 131104 | tf_op jit(solution)/shard_map/ppermute | solution.py:20
  138.6 10.8 %gather_fusion.4 = f32[4096,128]{1,0:T(8,128)S(1)} fusion(f32[768,128]{1,0:T(8,128)S(1)} %pad_maximum_fusion.4, s32[4096]{0:T(1024)S(1)} %fusion.4), kind=kCustom, calls=%fused_computation.4.clone | custom fusion | bytes 4210688 | tf_op jit(solution)/shard_map/jit(_take)/gather | solution.py:57
  149.4 2.1 broadcast_select_fusion.3
  154.9 5.3 %collective-permute-done.10 = f32[256,128]{1,0:T(8,128)S(1)} collective-permute-done((f32[256,128]{1,0:T(8,128)S(1)}, f32[256,128]{1,0:T(8,128)S(1)}, u32[]{:S(2)}, u32[]{:S(2)}) %collective-permute-start.10) | collective-permute-done | bytes 131104 | tf_op jit(solution)/shard_map/ppermute | solution.py:20
  160.2 10.8 %gather_fusion.5 = f32[4096,128]{1,0:T(8,128)S(1)} fusion(f32[768,128]{1,0:T(8,128)S(1)} %pad_maximum_fusion.5, s32[4096]{0:T(1024)S(1)} %fusion.4), kind=kCustom, calls=%fused_computation.5.clone | custom fusion | bytes 4210688 | tf_op jit(solution)/shard_map/jit(_take)/gather | solution.py:57
  171.0 2.1 broadcast_select_fusion.2
  176.5 5.3 %collective-permute-done.12 = f32[256,128]{1,0:T(8,128)S(1)} collective-permute-done((f32[256,128]{1,0:T(8,128)S(1)}, f32[256,128]{1,0:T(8,128)S(1)}, u32[]{:S(2)}, u32[]{:S(2)}) %collective-permute-start.12) | collective-permute-done | bytes 131104 | tf_op jit(solution)/shard_map/ppermute | solution.py:20
  181.8 10.8 %gather_fusion.6 = f32[4096,128]{1,0:T(8,128)S(1)} fusion(f32[768,128]{1,0:T(8,128)S(1)} %pad_maximum_fusion.6, s32[4096]{0:T(1024)S(1)} %fusion.4), kind=kCustom, calls=%fused_computation.6.clone | custom fusion | bytes 4210688 | tf_op jit(solution)/shard_map/jit(_take)/gather | solution.py:57
  192.5 2.1 broadcast_select_fusion.1
  198.0 5.3 %collective-permute-done.14 = f32[256,128]{1,0:T(8,128)S(1)} collective-permute-done((f32[256,128]{1,0:T(8,128)S(1)}, f32[256,128]{1,0:T(8,128)S(1)}, u32[]{:S(2)}, u32[]{:S(2)}) %collective-permute-start.14) | collective-permute-done | bytes 131104 | tf_op jit(solution)/shard_map/ppermute | solution.py:20
  203.3 10.8 %gather_fusion.7 = f32[4096,128]{1,0:T(8,128)S(1)} fusion(f32[768,128]{1,0:T(8,128)S(1)} %pad_maximum_fusion.7, s32[4096]{0:T(1024)S(1)} %fusion.4), kind=kCustom, calls=%fused_computation.7.clone | custom fusion | bytes 4210688 | tf_op jit(solution)/shard_map/jit(_take)/gather | solution.py:57
  214.1 2.1 broadcast_select_fusion
  (88 shorter events, 28.4 us)
Async XLA Ops:
  0.6 0.8 copy-start
  0.6 12.8 %copy-start.5 = (f32[128,256]{1,0:T(8,128)S(1)}, f32[128,256]{1,0:T(8,128)}, u32[]{:S(2)}) copy-start(f32[128,256]{1,0:T(8,128)} %param.10) | copy-start | bytes 393220
  0.7 12.9 %copy-start.10 = (s32[128]{0:T(128)S(1)}, s32[128]{0:T(128)}, u32[]{:S(2)}) copy-start(s32[128]{0:T(128)} %param.11) | copy-start | bytes 1540
  1.5 17.2 %copy-start.7 = (s32[16,256]{1,0:T(8,128)S(1)}, s32[16,256]{1,0:T(8,128)}, u32[]{:S(2)}) copy-start(s32[16,256]{1,0:T(8,128)} %param.12) | copy-start | bytes 49156
  6.1 18.9 %all-to-all-start = ((f32[32,16,256]{2,1,0:T(8,128)}), f32[32,16,256]{2,1,0:T(8,128)S(1)}, u32[]{:S(2)}, u32[]{:S(2)}) async-start(f32[32,16,256]{2,1,0:T(8,128)} %copy.26), calls=%async_computation | async-start | bytes 1048576 | tf_op jit(solution)/shard_map/all_to_all | solution.py:37
  13.7 20.7 %collective-permute-start.1 = (f32[256,128]{1,0:T(8,128)S(1)}, f32[256,128]{1,0:T(8,128)S(1)}, u32[]{:S(2)}, u32[]{:S(2)}) collective-permute-start(f32[256,128]{1,0:T(8,128)S(1)} %bitcast_select_fusion), channel_id=1, source_target_pairs={{1,0},{2,1},{3,2},{4,3},{5,4},{6,5},{7,6},{8,7},{9,8},{10,9},{11,1... | collective-permute-start | bytes 393224 | tf_op jit(solution)/shard_map/ppermute | solution.py:22
  18.7 15.7 %collective-permute-start = (f32[256,128]{1,0:T(8,128)S(1)}, f32[256,128]{1,0:T(8,128)S(1)}, u32[]{:S(2)}, u32[]{:S(2)}) collective-permute-start(f32[256,128]{1,0:T(8,128)S(1)} %bitcast_select_fusion), channel_id=1, source_target_pairs={{0,1},{1,2},{2,3},{3,4},{4,5},{5,6},{6,7},{7,8},{8,9},{9,10},{10,1... | collective-permute-start | bytes 393224 | tf_op jit(solution)/shard_map/ppermute | solution.py:20
  25.7 22.7 %all-to-all-start.1 = ((f32[8,16,256]{2,1,0:T(8,128)}), f32[8,16,256]{2,1,0:T(8,128)S(1)}, u32[]{:S(2)}, u32[]{:S(2)}) async-start(f32[8,16,256]{2,1,0:T(8,128)} %broadcast_in_dim.27), calls=%async_computation.1 | async-start | bytes 262144 | tf_op jit(solution)/shard_map/all_to_all | solution.py:43
  34.4 14.1 %copy-start.6 = (f32[16,256]{1,0:T(8,128)S(1)}, f32[16,256]{1,0:T(8,128)}, u32[]{:S(2)}) copy-start(f32[16,256]{1,0:T(8,128)} %param.15) | copy-start | bytes 49156
  50.4 11.4 %all-to-all-start.2 = ((f32[32,1,1]{2,1,0:T(1,128)}), f32[32,1,1]{2,1,0:T(1,128)S(1)}, u32[]{:S(2)}, u32[]{:S(2)}) async-start(f32[32,1,1]{2,1,0:T(1,128)} %broadcast_in_dim.28), calls=%async_computation.2 | async-start | bytes 32768 | tf_op jit(solution)/shard_map/all_to_all | solution.py:43
  54.5 8.6 %copy-start.8 = (f32[16,256]{1,0:T(8,128)S(1)}, f32[16,256]{1,0:T(8,128)}, u32[]{:S(2)}) copy-start(f32[16,256]{1,0:T(8,128)} %param.14) | copy-start | bytes 49156
  54.5 8.6 %copy-start.9 = (f32[16,256]{1,0:T(8,128)S(1)}, f32[16,256]{1,0:T(8,128)}, u32[]{:S(2)}) copy-start(f32[16,256]{1,0:T(8,128)} %param.13) | copy-start | bytes 49156
  64.5 20.0 %copy-start.3 = (f32[256,128]{1,0:T(8,128)}, f32[256,128]{1,0:T(8,128)S(1)}, u32[]{:S(2)}) copy-start(f32[256,128]{1,0:T(8,128)S(1)} %add_reduce_fusion.7) | copy-start | bytes 393220
  64.6 3.9 %collective-permute-start.3 = (f32[256,128]{1,0:T(8,128)S(1)}, f32[256,128]{1,0:T(8,128)S(1)}, u32[]{:S(2)}, u32[]{:S(2)}) collective-permute-start(f32[256,128]{1,0:T(8,128)S(1)} %fusion.5), channel_id=1, source_target_pairs={{1,0},{2,1},{3,2},{4,3},{5,4},{6,5},{7,6},{8,7},{9,8},{10,9},{11,1... | collective-permute-start | bytes 393224 | tf_op jit(solution)/shard_map/ppermute | solution.py:22
  65.9 7.7 %collective-permute-start.2 = (f32[256,128]{1,0:T(8,128)S(1)}, f32[256,128]{1,0:T(8,128)S(1)}, u32[]{:S(2)}, u32[]{:S(2)}) collective-permute-start(f32[256,128]{1,0:T(8,128)S(1)} %fusion.5), channel_id=1, source_target_pairs={{0,1},{1,2},{2,3},{3,4},{4,5},{5,6},{6,7},{7,8},{8,9},{9,10},{10,1... | collective-permute-start | bytes 393224 | tf_op jit(solution)/shard_map/ppermute | solution.py:20
  87.4 2.6 %collective-permute-start.5 = (f32[256,128]{1,0:T(8,128)S(1)}, f32[256,128]{1,0:T(8,128)S(1)}, u32[]{:S(2)}, u32[]{:S(2)}) collective-permute-start(f32[256,128]{1,0:T(8,128)S(1)} %min.49), channel_id=1, source_target_pairs={{1,0},{2,1},{3,2},{4,3},{5,4},{6,5},{7,6},{8,7},{9,8},{10,9},{11,1... | collective-permute-start | bytes 393224 | tf_op jit(solution)/shard_map/ppermute | solution.py:22
  87.5 7.8 %collective-permute-start.4 = (f32[256,128]{1,0:T(8,128)S(1)}, f32[256,128]{1,0:T(8,128)S(1)}, u32[]{:S(2)}, u32[]{:S(2)}) collective-permute-start(f32[256,128]{1,0:T(8,128)S(1)} %min.49), channel_id=1, source_target_pairs={{0,1},{1,2},{2,3},{3,4},{4,5},{5,6},{6,7},{7,8},{8,9},{9,10},{10,1... | collective-permute-start | bytes 393224 | tf_op jit(solution)/shard_map/ppermute | solution.py:20
  108.9 2.8 %collective-permute-start.7 = (f32[256,128]{1,0:T(8,128)S(1)}, f32[256,128]{1,0:T(8,128)S(1)}, u32[]{:S(2)}, u32[]{:S(2)}) collective-permute-start(f32[256,128]{1,0:T(8,128)S(1)} %min.51), channel_id=1, source_target_pairs={{1,0},{2,1},{3,2},{4,3},{5,4},{6,5},{7,6},{8,7},{9,8},{10,9},{11,1... | collective-permute-start | bytes 393224 | tf_op jit(solution)/shard_map/ppermute | solution.py:22
  109.2 7.8 %collective-permute-start.6 = (f32[256,128]{1,0:T(8,128)S(1)}, f32[256,128]{1,0:T(8,128)S(1)}, u32[]{:S(2)}, u32[]{:S(2)}) collective-permute-start(f32[256,128]{1,0:T(8,128)S(1)} %min.51), channel_id=1, source_target_pairs={{0,1},{1,2},{2,3},{3,4},{4,5},{5,6},{6,7},{7,8},{8,9},{9,10},{10,1... | collective-permute-start | bytes 393224 | tf_op jit(solution)/shard_map/ppermute | solution.py:20
  130.7 2.6 %collective-permute-start.9 = (f32[256,128]{1,0:T(8,128)S(1)}, f32[256,128]{1,0:T(8,128)S(1)}, u32[]{:S(2)}, u32[]{:S(2)}) collective-permute-start(f32[256,128]{1,0:T(8,128)S(1)} %min.53), channel_id=1, source_target_pairs={{1,0},{2,1},{3,2},{4,3},{5,4},{6,5},{7,6},{8,7},{9,8},{10,9},{11,1... | collective-permute-start | bytes 393224 | tf_op jit(solution)/shard_map/ppermute | solution.py:22
  130.8 7.8 %collective-permute-start.8 = (f32[256,128]{1,0:T(8,128)S(1)}, f32[256,128]{1,0:T(8,128)S(1)}, u32[]{:S(2)}, u32[]{:S(2)}) collective-permute-start(f32[256,128]{1,0:T(8,128)S(1)} %min.53), channel_id=1, source_target_pairs={{0,1},{1,2},{2,3},{3,4},{4,5},{5,6},{6,7},{7,8},{8,9},{9,10},{10,1... | collective-permute-start | bytes 393224 | tf_op jit(solution)/shard_map/ppermute | solution.py:20
  152.3 2.6 %collective-permute-start.11 = (f32[256,128]{1,0:T(8,128)S(1)}, f32[256,128]{1,0:T(8,128)S(1)}, u32[]{:S(2)}, u32[]{:S(2)}) collective-permute-start(f32[256,128]{1,0:T(8,128)S(1)} %min.55), channel_id=1, source_target_pairs={{1,0},{2,1},{3,2},{4,3},{5,4},{6,5},{7,6},{8,7},{9,8},{10,9},{11,1... | collective-permute-start | bytes 393224 | tf_op jit(solution)/shard_map/ppermute | solution.py:22
  152.4 7.8 %collective-permute-start.10 = (f32[256,128]{1,0:T(8,128)S(1)}, f32[256,128]{1,0:T(8,128)S(1)}, u32[]{:S(2)}, u32[]{:S(2)}) collective-permute-start(f32[256,128]{1,0:T(8,128)S(1)} %min.55), channel_id=1, source_target_pairs={{0,1},{1,2},{2,3},{3,4},{4,5},{5,6},{6,7},{7,8},{8,9},{9,10},{10,1... | collective-permute-start | bytes 393224 | tf_op jit(solution)/shard_map/ppermute | solution.py:20
  173.8 7.9 %copy-start.1 = (f32[256,128]{1,0:T(8,128)}, f32[256,128]{1,0:T(8,128)S(1)}, u32[]{:S(2)}) copy-start(f32[256,128]{1,0:T(8,128)S(1)} %add_reduce_fusion.2) | copy-start | bytes 393220
  173.8 2.6 %collective-permute-start.13 = (f32[256,128]{1,0:T(8,128)S(1)}, f32[256,128]{1,0:T(8,128)S(1)}, u32[]{:S(2)}, u32[]{:S(2)}) collective-permute-start(f32[256,128]{1,0:T(8,128)S(1)} %min.57), channel_id=1, source_target_pairs={{1,0},{2,1},{3,2},{4,3},{5,4},{6,5},{7,6},{8,7},{9,8},{10,9},{11,1... | collective-permute-start | bytes 393224 | tf_op jit(solution)/shard_map/ppermute | solution.py:22
  173.9 7.8 %collective-permute-start.12 = (f32[256,128]{1,0:T(8,128)S(1)}, f32[256,128]{1,0:T(8,128)S(1)}, u32[]{:S(2)}, u32[]{:S(2)}) collective-permute-start(f32[256,128]{1,0:T(8,128)S(1)} %min.57), channel_id=1, source_target_pairs={{0,1},{1,2},{2,3},{3,4},{4,5},{5,6},{6,7},{7,8},{8,9},{9,10},{10,1... | collective-permute-start | bytes 393224 | tf_op jit(solution)/shard_map/ppermute | solution.py:20
  195.4 2.6 %collective-permute-start.15 = (f32[256,128]{1,0:T(8,128)S(1)}, f32[256,128]{1,0:T(8,128)S(1)}, u32[]{:S(2)}, u32[]{:S(2)}) collective-permute-start(f32[256,128]{1,0:T(8,128)S(1)} %min.59), channel_id=1, source_target_pairs={{1,0},{2,1},{3,2},{4,3},{5,4},{6,5},{7,6},{8,7},{9,8},{10,9},{11,1... | collective-permute-start | bytes 393224 | tf_op jit(solution)/shard_map/ppermute | solution.py:22
  195.5 7.8 %collective-permute-start.14 = (f32[256,128]{1,0:T(8,128)S(1)}, f32[256,128]{1,0:T(8,128)S(1)}, u32[]{:S(2)}, u32[]{:S(2)}) collective-permute-start(f32[256,128]{1,0:T(8,128)S(1)} %min.59), channel_id=1, source_target_pairs={{0,1},{1,2},{2,3},{3,4},{4,5},{5,6},{6,7},{7,8},{8,9},{9,10},{10,1... | collective-permute-start | bytes 393224 | tf_op jit(solution)/shard_map/ppermute | solution.py:20
  216.3 0.9 copy-start.2
  216.3 1.0 copy-start.4
where the time goes:
time: 219 us; the launch traced here: 218 us
  local copies, waits for them, and re-layouts  93.9 us (43%)
  waiting for transfers between devices  61.4 us (28%)
  other arithmetic  30.9 us (14%)
  starting transfers between devices  30 us (14%)
    gather x8, local copies, waits for them, and re-layouts, relax(): jnp.take(window, local_index, axis=0)  89.5 us
    ppermute x8, waiting for transfers between devices, with_halo(): lax.ppermute(tail, axis, [(i, (i + 1) % count) for i in range(count)])  36.8 us
    select_n x8, other arithmetic, relax(): jnp.take(window, local_index, axis=0)  18.6 us
    ppermute x8, waiting for transfers between devices, with_halo(): lax.ppermute(head, axis, [((i + 1) % count, i) for i in range(count)])  14.6 us
    all_to_all x2, starting transfers between devices, copy_for_each(): lax.all_to_all(jnp.broadcast_to(array[None], (size, *array.shape)), axis,...  12.7 us
    all_to_all x1, starting transfers between devices, sent_and_summed(): lax.all_to_all(tiles, axis, split_axis=0, concat_axis=0, tiled=True)  7.32 us
    ppermute x8, starting transfers between devices, with_halo(): lax.ppermute(head, axis, [((i + 1) % count, i) for i in range(count)])  7.03 us
    all_to_all x1, waiting for transfers between devices, sent_and_summed(): lax.all_to_all(tiles, axis, split_axis=0, concat_axis=0, tiled=True)  6.3 us
  transfers between devices with their start and end apart: 19, of which 16 were waited for; matrix products, arithmetic and copies ran while one was open for 9% of the time, Pallas kernels for 0%

commit v1 on v0

v1 whole, which is shorter than its diff:
```python
import functools

import jax
import jax.numpy as jnp
from jax import lax
from jax.experimental import pallas as pl
from jax.experimental.pallas import tpu as pltpu
from jax.sharding import PartitionSpec as P

SWEEPS = 8
LANES = 128
MESH = pl.DeviceIdType.MESH
F32 = jnp.float32
BF16 = jnp.bfloat16

step_size = 0.25
eps_value = 1e-06


def parts(x):
    high = x.astype(BF16)
    return high, (x - high.astype(F32)).astype(BF16)


def peer_of(axis, size, step):
    return lax.rem(lax.axis_index(axis) + step, size)


def kernel(
    arcs, comms, nodes,
    dist_ref, source_ref, tail_ref, cost_ref, price_ref, cap_ref, path_ref, demand_ref,
    dist_out, price_out,
    own, left, right, best, lhs, hot, rel, weight,
    pay, routes, ends, picks, flow, flows, square, squares,
    near_send, near_recv, pay_send, pay_recv, flow_send, flow_recv, square_send, square_recv,
):
    me = lax.axis_index("arc")
    group = lax.axis_index("comm")
    span = 2 * LANES
    first = me * span
    after = lax.rem(me + 1, arcs)
    before = lax.rem(me + arcs - 1, arcs)

    barrier = pltpu.get_barrier_semaphore()

    @pl.loop(1, arcs)
    def _(step):
        pl.semaphore_signal(
            barrier, inc=1, device_id={"arc": peer_of("arc", arcs, step)}, device_id_type=MESH
        )

    @pl.loop(1, comms)
    def _(step):
        pl.semaphore_signal(
            barrier, inc=1, device_id={"comm": peer_of("comm", comms, step)}, device_id_type=MESH
        )

    source = jnp.broadcast_to(source_ref[...], (LANES, LANES)).T
    lane = lax.broadcasted_iota(jnp.int32, (LANES, LANES), 1)
    for b in range(2):
        block = dist_ref[:, b * LANES : (b + 1) * LANES]
        own[0, b] = jnp.where(source == lane + (first + b * LANES), F32(0.0), block)

    pay[0:4, :] = path_ref[...].astype(F32)
    for r in range(4):
        pay[4 + r : 5 + r, :] = jnp.full((1, LANES), demand_ref[r], F32)

    arc_weight = cost_ref[...] + price_ref[...]
    shifted = tail_ref[...] - (first - span)
    shifted = jnp.where(shifted < 0, shifted + nodes, shifted)
    shifted = jnp.where(shifted >= nodes, shifted - nodes, shifted)
    for h in range(2):
        cols = slice(h * LANES, (h + 1) * LANES)
        pair = jnp.concatenate([shifted[0:8, cols], shifted[8:16, cols]], axis=1)
        cost = jnp.concatenate([arc_weight[0:8, cols], arc_weight[8:16, cols]], axis=1)
        rel[h] = pair
        at = pair // LANES
        inside = (at == 2) | (at == 3)
        near = (at == 1) | (at == 4)
        weight[0, h] = jnp.where(inside, cost, jnp.inf)
        weight[1, h] = jnp.where(near, cost, jnp.inf)
        weight[2, h] = jnp.where(inside | near, jnp.inf, cost)

    row = lax.broadcasted_iota(jnp.int32, (LANES, span), 0)

    @pl.loop(0, 8)
    def _(t):
        for h in range(2):
            want = jnp.broadcast_to(rel[h, pl.ds(t, 1), :], (LANES, span))
            for k, at in enumerate((2, 3, 1, 4, 0 if h == 0 else 5)):
                one = jnp.where(want == row + at * LANES, F32(1.0), F32(0.0)).astype(BF16)
                hot[h, t, k * span : k * span + LANES, :] = one
                hot[h, t, k * span + LANES : (k + 1) * span, :] = one

    pl.semaphore_wait(barrier, arcs + comms - 2)

    def near_copies(slot):
        out = []
        for k, (b, there, target) in enumerate(
            ((1, left, after), (0, right, before), (0, left, after), (1, right, before))
        ):
            out.append(
                pltpu.make_async_remote_copy(
                    src_ref=own.at[slot, b],
                    dst_ref=there.at[slot, b],
                    send_sem=near_send.at[slot, k],
                    recv_sem=near_recv.at[slot, k],
                    device_id={"arc": target},
                    device_id_type=MESH,
                )
            )
        return out

    def spread(axis, size, source_ref_, target_ref, send, recv):
        mine = lax.axis_index(axis)

        def copy(peer, slot):
            return pltpu.make_async_remote_copy(
                src_ref=source_ref_,
                dst_ref=target_ref.at[slot],
                send_sem=send.at[peer],
                recv_sem=recv.at[slot],
                device_id={axis: peer},
                device_id_type=MESH,
            )

        def start():
            @pl.loop(1, size)
            def _(step):
                copy(peer_of(axis, size, step), mine).start()

        def finish():
            @pl.loop(1, size)
            def _(step):
                peer = peer_of(axis, size, step)
                copy(peer, mine).wait_send()
                copy(peer, peer).wait_recv()

        return start, finish

    send_pay, get_pay = spread("arc", arcs, pay, routes, pay_send, pay_recv)
    send_flow, get_flow = spread("comm", comms, flow, flows, flow_send, flow_recv)
    send_square, get_square = spread("arc", arcs, square, squares, square_send, square_recv)

    def phase(p, h, start, width, best_dist):
        cols = slice(start, start + width)
        rows = slice((0, 512, 1024)[p], (0, 512, 1024)[p] + width)
        for t in range(8):
            found = jnp.dot(lhs[:, cols], hot[h, t, rows, :], preferred_element_type=F32)
            found = found + weight[p, h, t : t + 1, :]
            best_dist = jnp.minimum(best_dist, jnp.minimum(found[:, :LANES], found[:, LANES:]))
        return best_dist

    def put(place, block):
        high, low = parts(block)
        lhs[:, place * span : place * span + LANES] = high
        lhs[:, place * span + LANES : (place + 1) * span] = low

    def histogram():
        get_pay()
        routes[me] = pay[...]
        node_row = lax.broadcasted_iota(jnp.int32, (span, LANES), 0)
        slot_row = lax.broadcasted_iota(jnp.int32, (16, LANES), 0)

        def chunk(c, total):
            for i in range(8):
                for r in range(4):
                    at = slice((i * 4 + r) * LANES, (i * 4 + r + 1) * LANES)
                    ids = routes[c * 8 + i, r : r + 1, :].astype(jnp.int32)
                    amount = routes[c * 8 + i, 4 + r : 5 + r, :]
                    node = jnp.broadcast_to((ids & (nodes - 1)) - first, (span, LANES))
                    hop_slot = jnp.broadcast_to(ids // nodes, (16, LANES))
                    ends[:, at] = jnp.where(node == node_row, F32(1.0), F32(0.0)).astype(BF16)
                    given = jnp.where(hop_slot == slot_row, amount, F32(0.0))
                    high, low = parts(given)
                    picks[0:16, at] = high
                    picks[16:32, at] = low
            return total + lax.dot_general(
                picks[...], ends[...], (((1,), (1,)), ((), ())), preferred_element_type=F32
            )

        total = lax.fori_loop(0, arcs // 8, chunk, jnp.zeros((32, span), F32))
        flow[...] = total[0:16] + total[16:32]
        flows[group] = flow[...]
        send_flow()

    def squares_out():
        get_flow()
        total = flows[0]
        for z in range(1, comms):
            total = total + flows[z]
        gradient = total - cap_ref[...]
        flow[...] = gradient
        sq = gradient * gradient
        square[...] = (sq[0:8, :LANES] + sq[8:16, :LANES]) + (sq[0:8, LANES:] + sq[8:16, LANES:])
        squares[me] = square[...]
        send_square()

    def prices():
        get_square()
        total = squares[0]
        for a in range(1, arcs):
            total = total + squares[a]
        whole = jnp.sum(total, axis=(0, 1), keepdims=True)
        root = jnp.sqrt(whole / F32(16 * nodes) + F32(eps_value))
        price_out[...] = jnp.maximum(
            price_ref[...] + F32(step_size) * flow[...] / root, F32(0.0)
        )

    @pl.loop(0, SWEEPS)
    def _(sweep):
        slot = lax.rem(sweep, 2)
        copies = near_copies(slot)
        for copy in copies:
            copy.start()
        pl.when(sweep == 0)(send_pay)
        for b in range(2):
            put(b, own[slot, b])
        for h in range(2):
            best[h] = phase(0, h, 0, 512, own[slot, h])
        pl.when(sweep == 1)(histogram)
        pl.when(sweep == 3)(squares_out)
        pl.when(sweep == 5)(prices)
        copies[0].wait_recv()
        copies[1].wait_recv()
        put(2, left[slot, 1])
        put(3, right[slot, 0])
        for h in range(2):
            best[h] = phase(1, h, 512, 512, best[h])
        copies[2].wait_recv()
        copies[3].wait_recv()
        put(4, left[slot, 0])
        put(5, right[slot, 1])
        for copy in copies:
            copy.wait_send()
        for h in range(2):
            own[1 - slot, h] = phase(2, h, 1024 + h * span, span, best[h])

    for b in range(2):
        dist_out[:, b * LANES : (b + 1) * LANES] = own[SWEEPS % 2, b]


def shards(prev_dist, source_node, arc_tail, base_cost, arc_price, capacity, path_arcs, demand):
    arcs = lax.axis_size("arc")
    comms = lax.axis_size("comm")
    rows, span = prev_dist.shape
    vmem = pl.BlockSpec(memory_space=pltpu.VMEM)
    smem = pl.BlockSpec(memory_space=pltpu.SMEM)
    dma = pltpu.SemaphoreType.DMA
    return pl.pallas_call(
        functools.partial(kernel, arcs, comms, arcs * span),
        out_shape=(
            jax.ShapeDtypeStruct(prev_dist.shape, F32),
            jax.ShapeDtypeStruct(arc_price.shape, F32),
        ),
        in_specs=[vmem] * 7 + [smem],
        out_specs=(vmem, vmem),
        scratch_shapes=[
            pltpu.VMEM((2, 2, rows, LANES), F32),
            pltpu.VMEM((2, 2, rows, LANES), F32),
            pltpu.VMEM((2, 2, rows, LANES), F32),
            pltpu.VMEM((2, rows, LANES), F32),
            pltpu.VMEM((rows, 12 * LANES), BF16),
            pltpu.VMEM((2, 8, 10 * LANES, span), BF16),
            pltpu.VMEM((2, 8, span), jnp.int32),
            pltpu.VMEM((3, 2, 8, span), F32),
            pltpu.VMEM((8, LANES), F32),
            pltpu.VMEM((arcs, 8, LANES), F32),
            pltpu.VMEM((span, 32 * LANES), BF16),
            pltpu.VMEM((32, 32 * LANES), BF16),
            pltpu.VMEM((16, span), F32),
            pltpu.VMEM((comms, 16, span), F32),
            pltpu.VMEM((8, LANES), F32),
            pltpu.VMEM((arcs, 8, LANES), F32),
            dma((2, 4)),
            dma((2, 4)),
            dma((arcs,)),
            dma((arcs,)),
            dma((comms,)),
            dma((comms,)),
            dma((arcs,)),
            dma((arcs,)),
        ],
        compiler_params=pltpu.CompilerParams(
            collective_id=0, has_side_effects=True, vmem_limit_bytes=48 * 1024 * 1024
        ),
    )(
        prev_dist, source_node.reshape(1, rows), arc_tail, base_cost, arc_price, capacity,
        path_arcs, demand,
    )


def solution(mesh):
    in_specs = (
        P("comm", "arc"),
        P("comm"),
        P(None, "arc"),
        P(None, "arc"),
        P(None, "arc"),
        P(None, "arc"),
        P(("comm", "arc"), None),
        P(("comm", "arc")),
    )
    out_specs = (P("comm", "arc"), P(None, "arc"))
    return jax.shard_map(shards, mesh=mesh, in_specs=in_specs, out_specs=out_specs, check_vma=False)
```

time: 219 us -> 66 us (0.30)
  local copies, waits for them, and re-layouts: 93.9 us -> 6.37 us
  waiting for transfers between devices: 61.4 us -> 0 us
  Pallas kernels: 0 us -> 58.5 us
  other arithmetic: 30.9 us -> 0 us
  starting transfers between devices: 30 us -> 0 us
    gather x8 -> x0, local copies, waits for them, and re-layouts: 89.5 us -> none  [relax(): jnp.take(window, local_index, axis=0)]
    pallas_call x0 -> x1, Pallas kernels: none -> 58.5 us  [shards(): pl.pallas_call(functools.partial(kernel, arcs, comms, arcs * span), out_s...]
    ppermute x16 -> x0, waiting for transfers between devices: 51.5 us -> none  [the longest x8 36.8 us: with_halo(): lax.ppermute(tail, axis, [(i, (i + 1) % count) for i in range(count)])]
    all_to_all x3 -> x0, starting transfers between devices: 20 us -> none  [the longest x2 12.7 us: copy_for_each(): lax.all_to_all(jnp.broadcast_to(array[None], (size, *array.shape)), axis,...]
    select_n x10 -> x0, other arithmetic: 19.4 us -> none  [the longest x8 18.6 us: relax(): jnp.take(window, local_index, axis=0)]
    ppermute x16 -> x0, starting transfers between devices: 10 us -> none  [the longest x8 7.03 us: with_halo(): lax.ppermute(head, axis, [((i + 1) % count, i) for i in range(count)])]
    all_to_all x3 -> x0, waiting for transfers between devices: 9.96 us -> none  [the longest x1 6.3 us: sent_and_summed(): lax.all_to_all(tiles, axis, split_axis=0, concat_axis=0, tiled=True)]
    reduce_min x8 -> x0, other arithmetic: 5.62 us -> none  [relax(): return jnp.minimum(current, jnp.min(candidate, axis=0))]
  transfers between devices with their start and end apart: 19 -> 0, of which waited for: 16 -> 0; matrix products, arithmetic and copies ran while one was open for 9% -> 0% of each run, Pallas kernels for 0% -> 0%
where the time goes in v1:
time: 66 us; the launch traced here: 65.5 us
  Pallas kernels  58.5 us (89%)
  local copies, waits for them, and re-layouts  6.37 us (10%)
  between operations  0.66 us (1%)
    pallas_call x1, Pallas kernels, shards(): pl.pallas_call(functools.partial(kernel, arcs, comms, arcs * span), out_s...  58.5 us
    unnamed x18, local copies, waits for them, and re-layouts  6.37 us

profile of v1, /device:TPU:32, one launch (start us, length us, event | category | flops | bytes accessed | tf_op | source)
XLA Modules:
  0.0 65.5 jit_solution(4662835140222268031)
XLA Ops:
  0.6 0.0 copy-start.7
  0.6 0.0 copy-start.6
  0.7 0.6 copy-done.7
  1.3 0.0 copy-done.6
  1.3 0.0 copy-start
  1.3 0.9 %copy-done = f32[128,256]{1,0:T(8,128)S(1)} copy-done((f32[128,256]{1,0:T(8,128)S(1)}, f32[128,256]{1,0:T(8,128)}, u32[]{:S(2)}) %copy-start) | copy-done | bytes 131096
  2.2 0.0 copy-start.1
  2.2 0.7 %copy-done.1 = s32[16,256]{1,0:T(8,128)S(1)} copy-done((s32[16,256]{1,0:T(8,128)S(1)}, s32[16,256]{1,0:T(8,128)}, u32[]{:S(2)}) %copy-start.1) | copy-done | bytes 16408
  2.9 0.0 copy-start.2
  2.9 0.7 %copy-done.2 = f32[16,256]{1,0:T(8,128)S(1)} copy-done((f32[16,256]{1,0:T(8,128)S(1)}, f32[16,256]{1,0:T(8,128)}, u32[]{:S(2)}) %copy-start.2) | copy-done | bytes 16408
  3.6 0.0 copy-start.3
  3.6 0.7 %copy-done.3 = f32[16,256]{1,0:T(8,128)S(1)} copy-done((f32[16,256]{1,0:T(8,128)S(1)}, f32[16,256]{1,0:T(8,128)}, u32[]{:S(2)}) %copy-start.3) | copy-done | bytes 16408
  4.4 0.0 copy-start.4
  4.4 0.7 %copy-done.4 = f32[16,256]{1,0:T(8,128)S(1)} copy-done((f32[16,256]{1,0:T(8,128)S(1)}, f32[16,256]{1,0:T(8,128)}, u32[]{:S(2)}) %copy-start.4) | copy-done | bytes 16408
  5.1 0.0 copy-start.5
  5.1 0.7 %copy-done.5 = s32[4,128]{1,0:T(4,128)S(1)} copy-done((s32[4,128]{1,0:T(4,128)S(1)}, s32[4,128]{1,0:T(4,128)}, u32[]{:S(2)}) %copy-start.5) | copy-done | bytes 2072
  5.8 58.5 %shard_map.95 = (f32[128,256]{1,0:T(8,128)S(1)}, f32[16,256]{1,0:T(8,128)S(1)}) custom-call(f32[128,256]{1,0:T(8,128)S(1)} %copy-done, s32[1,128]{1,0:T(1,128)S(1)} %bitcast.1, s32[16,256]{1,0:T(8,128)S(1)} %copy-done.1, f32[16,256]{1,0:T(8,128)S(1)} %copy-done.2, f32[16,256]{1,0:T(8,128)S(1)} %copy-done.3, f32[16,256]{1,0:T(8,128)S(1)} %copy-done.4, ...), custom_call_target="tpu_custom_call" | custom-call | tf_op jit(solution)/shard_map/pallas_call | solution.py:250
  64.3 0.7 %copy.12 = f32[128,256]{1,0:T(8,128)} copy(f32[128,256]{1,0:T(8,128)S(1)} %get-tuple-element.4) | data formatting | bytes 262144
  64.9 0.6 copy.13
Async XLA Ops:
  0.6 0.7 %copy-start.7 = (f32[4]{0:T(128)S(1)}, f32[4]{0:T(128)}, u32[]{:S(2)}) copy-start(f32[4]{0:T(128)} %demand_ref.1) | copy-start | bytes 52
  0.6 0.7 %copy-start.6 = (s32[128]{0:T(128)S(1)}, s32[128]{0:T(128)}, u32[]{:S(2)}) copy-start(s32[128]{0:T(128)} %param.9) | copy-start | bytes 1540
  1.3 0.9 %copy-start = (f32[128,256]{1,0:T(8,128)S(1)}, f32[128,256]{1,0:T(8,128)}, u32[]{:S(2)}) copy-start(f32[128,256]{1,0:T(8,128)} %dist_ref.1) | copy-start | bytes 393220
  2.2 0.7 %copy-start.1 = (s32[16,256]{1,0:T(8,128)S(1)}, s32[16,256]{1,0:T(8,128)}, u32[]{:S(2)}) copy-start(s32[16,256]{1,0:T(8,128)} %tail_ref.1) | copy-start | bytes 49156
  2.9 0.7 %copy-start.2 = (f32[16,256]{1,0:T(8,128)S(1)}, f32[16,256]{1,0:T(8,128)}, u32[]{:S(2)}) copy-start(f32[16,256]{1,0:T(8,128)} %cost_ref.1) | copy-start | bytes 49156
  3.6 0.7 %copy-start.3 = (f32[16,256]{1,0:T(8,128)S(1)}, f32[16,256]{1,0:T(8,128)}, u32[]{:S(2)}) copy-start(f32[16,256]{1,0:T(8,128)} %price_ref.1) | copy-start | bytes 49156
  4.4 0.7 %copy-start.4 = (f32[16,256]{1,0:T(8,128)S(1)}, f32[16,256]{1,0:T(8,128)}, u32[]{:S(2)}) copy-start(f32[16,256]{1,0:T(8,128)} %cap_ref.1) | copy-start | bytes 49156
  5.1 0.7 %copy-start.5 = (s32[4,128]{1,0:T(4,128)S(1)}, s32[4,128]{1,0:T(4,128)}, u32[]{:S(2)}) copy-start(s32[4,128]{1,0:T(4,128)} %path_ref.1) | copy-start | bytes 6148

commit v2 on v1

v2 whole, which is shorter than its diff:
```python
import functools

import jax
import jax.numpy as jnp
from jax import lax
from jax.experimental import pallas as pl
from jax.experimental.pallas import tpu as pltpu
from jax.sharding import PartitionSpec as P

SWEEPS = 8
CHUNKS = 2

LANES = 128
MESH = pl.DeviceIdType.MESH
F32 = jnp.float32
BF16 = jnp.bfloat16
HOT = jnp.float8_e4m3fn
ROW = 8

step_size = 0.25
eps_value = 1e-06


def parts(x):
    high = x.astype(BF16)
    return high, (x - high.astype(F32)).astype(BF16)


def kernel(
    arcs, comms, nodes,
    dist_hbm, source_hbm, tail_hbm, cost_hbm, price_hbm, cap_hbm, path_hbm, demand_ref,
    dist_out, price_out,
    dist_ref, source_ref, tail_ref, cost_ref, price_ref, cap_ref, path_ref, fetch_sem,
    own, left, right, best, lhs, hot, rel, weight,
    pay, routes, ends, picks, flow, flows, square, squares, square_sum, square_sums,
    near_send, near_recv, row_send, row_recv, col_send, col_recv, flow_send, flow_recv,
):
    me = lax.axis_index("arc")
    group = lax.axis_index("comm")
    span = 2 * LANES
    rows = LANES // CHUNKS
    first = me * span
    after = lax.rem(me + 1, arcs)
    before = lax.rem(me + arcs - 1, arcs)

    barrier = pltpu.get_barrier_semaphore()
    fetches = [
        pltpu.make_async_copy(there, here, fetch_sem.at[k])
        for k, (there, here) in enumerate(
            (
                (tail_hbm, tail_ref),
                (cost_hbm, cost_ref),
                (price_hbm, price_ref),
                (source_hbm, source_ref),
                (dist_hbm, dist_ref),
                (path_hbm, path_ref),
                (cap_hbm, cap_ref),
            )
        )
    ]
    for fetch in fetches:
        fetch.start()

    line = me // ROW
    place = lax.rem(me, ROW)
    lines = arcs // ROW

    def row_peer(step):
        return line * ROW + lax.rem(place + step, ROW)

    def col_peer(step):
        return lax.rem(line + step, lines) * ROW + place

    def ring(step):
        return lax.rem(group + comms + step, comms)

    greeted = [("arc", row_peer(step)) for step in range(1, ROW)]
    greeted += [("arc", col_peer(step)) for step in range(1, lines)]
    greeted += [("arc", after), ("arc", before)]
    greeted += [("comm", ring(step)) for step in (1, 2, -1, -2)]
    for axis, peer in greeted:
        pl.semaphore_signal(barrier, inc=1, device_id={axis: peer}, device_id_type=MESH)

    for fetch in fetches:
        fetch.wait()

    source = jnp.broadcast_to(source_ref[...], (LANES, LANES)).T
    lane = lax.broadcasted_iota(jnp.int32, (LANES, LANES), 1)
    for b in range(2):
        block = dist_ref[:, b * LANES : (b + 1) * LANES]
        block = jnp.where(source == lane + (first + b * LANES), F32(0.0), block)
        for c in range(CHUNKS):
            own[0, c, b] = block[c * rows : (c + 1) * rows]

    pay[0:4, :] = path_ref[...].astype(F32)
    for r in range(4):
        pay[4 + r : 5 + r, :] = jnp.full((1, LANES), demand_ref[r], F32)

    arc_weight = cost_ref[...] + price_ref[...]
    shifted = tail_ref[...] - (first - span)
    shifted = jnp.where(shifted < 0, shifted + nodes, shifted)
    shifted = jnp.where(shifted >= nodes, shifted - nodes, shifted)
    for h in range(2):
        cols = slice(h * LANES, (h + 1) * LANES)
        pair = jnp.concatenate([shifted[0:8, cols], shifted[8:16, cols]], axis=1)
        cost = jnp.concatenate([arc_weight[0:8, cols], arc_weight[8:16, cols]], axis=1)
        rel[h] = pair
        at = pair // LANES
        inside = (at == 2) | (at == 3)
        near = (at == 1) | (at == 4)
        weight[0, h] = jnp.where(inside, cost, jnp.inf)
        weight[1, h] = jnp.where(near, cost, jnp.inf)
        weight[2, h] = jnp.where(inside | near, jnp.inf, cost)

    row = lax.broadcasted_iota(jnp.int32, (LANES, span), 0)

    @pl.loop(0, 8)
    def _(t):
        for h in range(2):
            want = jnp.broadcast_to(rel[h, pl.ds(t, 1), :], (LANES, span))
            for k, at in enumerate((2, 3, 1, 4, 0 if h == 0 else 5)):
                one = jnp.where(want == row + at * LANES, F32(1.0), F32(0.0)).astype(HOT)
                hot[h, t, k * span : k * span + LANES, :] = one
                hot[h, t, k * span + LANES : (k + 1) * span, :] = one

    pl.semaphore_wait(barrier, len(greeted))

    def near_copies(slot, c):
        out = []
        for k, (b, there, target) in enumerate(
            ((1, left, after), (0, right, before), (0, left, after), (1, right, before))
        ):
            out.append(
                pltpu.make_async_remote_copy(
                    src_ref=own.at[slot, c, b],
                    dst_ref=there.at[slot, c, b],
                    send_sem=near_send.at[slot, c, k],
                    recv_sem=near_recv.at[slot, c, k],
                    device_id={"arc": target},
                    device_id_type=MESH,
                )
            )
        return out

    def row_copies(kind, source_at, target_at):
        return [
            pltpu.make_async_remote_copy(
                src_ref=source_at,
                dst_ref=target_at,
                send_sem=row_send.at[kind, step],
                recv_sem=row_recv.at[kind, step],
                device_id={"arc": row_peer(step)},
                device_id_type=MESH,
            )
            for step in range(1, ROW)
        ]

    def col_copies(kind, source_at, target_at):
        return [
            pltpu.make_async_remote_copy(
                src_ref=source_at,
                dst_ref=target_at,
                send_sem=col_send.at[kind, step],
                recv_sem=col_recv.at[kind, step],
                device_id={"arc": col_peer(step)},
                device_id_type=MESH,
            )
            for step in range(1, lines)
        ]

    def flow_copies(moves):
        return [
            pltpu.make_async_remote_copy(
                src_ref=flow if of is None else flows.at[ring(of)],
                dst_ref=flows.at[ring(0 if of is None else of)],
                send_sem=flow_send.at[k],
                recv_sem=flow_recv.at[k],
                device_id={"comm": ring(step)},
                device_id_type=MESH,
            )
            for k, of, step in moves
        ]

    mine = routes.at[pl.ds(pl.multiple_of(line * ROW, ROW), ROW)]
    row_pay = row_copies(0, pay, routes.at[me])
    col_pay = col_copies(0, mine, mine)
    near_flow = flow_copies([(0, None, 1), (1, None, 2), (2, None, -1), (3, None, -2)])
    far_flow = flow_copies([(4, 1, -2), (5, 2, -2), (6, -1, 2)])
    row_square = row_copies(1, square, squares.at[place])
    col_square = col_copies(1, square_sum, square_sums.at[line])

    def start(copies):
        for copy in copies:
            copy.start()

    def finish(copies):
        for copy in copies:
            copy.wait_send()
        for copy in copies:
            copy.wait_recv()

    def phase(p, c, h, start, width, best_dist):
        cols = slice(start, start + width)
        taken = slice((0, 512, 1024)[p], (0, 512, 1024)[p] + width)
        for t in range(8):
            found = jnp.dot(lhs[c, :, cols], hot[h, t, taken, :], preferred_element_type=F32)
            found = found + weight[p, h, t : t + 1, :]
            best_dist = jnp.minimum(best_dist, jnp.minimum(found[:, :LANES], found[:, LANES:]))
        return best_dist

    def put(c, place, block):
        high, low = parts(block)
        lhs[c, :, place * span : place * span + LANES] = high
        lhs[c, :, place * span + LANES : (place + 1) * span] = low

    def count_line(step):
        node_row = lax.broadcasted_iota(jnp.int32, (span, LANES), 0)
        slot_row = lax.broadcasted_iota(jnp.int32, (16, LANES), 0)
        base = lax.rem(line + step, lines) * ROW
        for i in range(ROW):
            for r in range(4):
                at = slice((i * 4 + r) * LANES, (i * 4 + r + 1) * LANES)
                ids = routes[base + i, r : r + 1, :].astype(jnp.int32)
                amount = routes[base + i, 4 + r : 5 + r, :]
                node = jnp.broadcast_to((ids & (nodes - 1)) - first, (span, LANES))
                hop_slot = jnp.broadcast_to(ids // nodes, (16, LANES))
                ends[:, at] = jnp.where(node == node_row, F32(1.0), F32(0.0)).astype(BF16)
                given = jnp.where(hop_slot == slot_row, amount, F32(0.0))
                high, low = parts(given)
                picks[0:16, at] = high
                picks[16:32, at] = low
        both = lax.dot_general(
            picks[...], ends[...], (((1,), (1,)), ((), ())), preferred_element_type=F32
        )
        return both[0:16] + both[16:32]

    def flow_step(t):
        if t == 0:
            finish(row_pay)
            routes[me] = pay[...]
            start(col_pay)
        if t == 1:
            flow[...] = count_line(0)
        if t == 2:
            finish(col_pay)

            @pl.loop(1, 3)
            def _(step):
                flow[...] += count_line(step)
        if t == 3:
            flow[...] += count_line(3)
            flows[group] = flow[...]
            start(near_flow)
        if t == 4:
            finish(near_flow)
            start(far_flow)
        if t == 5:
            finish(far_flow)
            total = flows[0]
            for z in range(1, comms):
                total = total + flows[z]
            gradient = total - cap_ref[...]
            flow[...] = gradient
            sq = gradient * gradient
            square[...] = (sq[0:8, :LANES] + sq[8:16, :LANES]) + (sq[0:8, LANES:] + sq[8:16, LANES:])
            start(row_square)
        if t == 6:
            finish(row_square)
            squares[place] = square[...]
            total = squares[0]
            for a in range(1, ROW):
                total = total + squares[a]
            square_sum[...] = total
            start(col_square)
        if t == 7:
            finish(col_square)
            square_sums[line] = square_sum[...]
            total = square_sums[0]
            for a in range(1, lines):
                total = total + square_sums[a]
            whole = jnp.sum(total, axis=(0, 1), keepdims=True)
            root = jnp.sqrt(whole / F32(16 * nodes) + F32(eps_value))
            price_out[...] = jnp.maximum(
                price_ref[...] + F32(step_size) * flow[...] / root, F32(0.0)
            )

    def send(slot, c):
        start(near_copies(slot, c))

    def inner(slot, c):
        for b in range(2):
            put(c, b, own[slot, c, b])
        for h in range(2):
            best[c, h] = phase(0, c, h, 0, 512, own[slot, c, h])

    def outer(slot, c):
        copies = near_copies(slot, c)
        copies[0].wait_recv()
        copies[1].wait_recv()
        put(c, 2, left[slot, c, 1])
        put(c, 3, right[slot, c, 0])
        for h in range(2):
            best[c, h] = phase(1, c, h, 512, 512, best[c, h])
        copies[2].wait_recv()
        copies[3].wait_recv()
        put(c, 4, left[slot, c, 0])
        put(c, 5, right[slot, c, 1])
        for copy in copies:
            copy.wait_send()
        for h in range(2):
            own[1 - slot, c, h] = phase(2, c, h, 1024 + h * span, span, best[c, h])

    for c in range(CHUNKS):
        send(0, c)
    start(row_pay)

    @pl.loop(0, SWEEPS)
    def _(sweep):
        slot = lax.rem(sweep, 2)
        for c in range(CHUNKS):
            inner(slot, c)
        for t in range(SWEEPS):
            pl.when(sweep == t)(functools.partial(flow_step, t))
        for c in range(CHUNKS):
            outer(slot, c)

            @pl.when(sweep < SWEEPS - 1)
            def _():
                send(1 - slot, c)

    for c in range(CHUNKS):
        for b in range(2):
            dist_out[c * rows : (c + 1) * rows, b * LANES : (b + 1) * LANES] = own[SWEEPS % 2, c, b]


def shards(prev_dist, source_node, arc_tail, base_cost, arc_price, capacity, path_arcs, demand):
    arcs = lax.axis_size("arc")
    comms = lax.axis_size("comm")
    rows, span = prev_dist.shape
    vmem = pl.BlockSpec(memory_space=pltpu.VMEM)
    smem = pl.BlockSpec(memory_space=pltpu.SMEM)
    dma = pltpu.SemaphoreType.DMA
    return pl.pallas_call(
        functools.partial(kernel, arcs, comms, arcs * span),
        out_shape=(
            pltpu.VMEM(prev_dist.shape, F32),
            pltpu.VMEM(arc_price.shape, F32),
        ),
        in_specs=[pl.BlockSpec(memory_space=pltpu.HBM)] * 7 + [smem],
        out_specs=(vmem, vmem),
        scratch_shapes=[
            pltpu.VMEM(prev_dist.shape, F32),
            pltpu.VMEM((1, rows), jnp.int32),
            pltpu.VMEM(arc_tail.shape, jnp.int32),
            pltpu.VMEM(arc_price.shape, F32),
            pltpu.VMEM(arc_price.shape, F32),
            pltpu.VMEM(arc_price.shape, F32),
            pltpu.VMEM(path_arcs.shape, jnp.int32),
            dma((7,)),
            pltpu.VMEM((2, CHUNKS, 2, rows // CHUNKS, LANES), F32),
            pltpu.VMEM((2, CHUNKS, 2, rows // CHUNKS, LANES), F32),
            pltpu.VMEM((2, CHUNKS, 2, rows // CHUNKS, LANES), F32),
            pltpu.VMEM((CHUNKS, 2, rows // CHUNKS, LANES), F32),
            pltpu.VMEM((CHUNKS, rows // CHUNKS, 12 * LANES), BF16),
            pltpu.VMEM((2, 8, 10 * LANES, span), HOT),
            pltpu.VMEM((2, 8, span), jnp.int32),
            pltpu.VMEM((3, 2, 8, span), F32),
            pltpu.VMEM((8, LANES), F32),
            pltpu.VMEM((arcs, 8, LANES), F32),
            pltpu.VMEM((span, 32 * LANES), BF16),
            pltpu.VMEM((32, 32 * LANES), BF16),
            pltpu.VMEM((16, span), F32),
            pltpu.VMEM((comms, 16, span), F32),
            pltpu.VMEM((8, LANES), F32),
            pltpu.VMEM((ROW, 8, LANES), F32),
            pltpu.VMEM((8, LANES), F32),
            pltpu.VMEM((arcs // ROW, 8, LANES), F32),
            dma((2, CHUNKS, 4)),
            dma((2, CHUNKS, 4)),
            dma((2, ROW)),
            dma((2, ROW)),
            dma((2, arcs // ROW)),
            dma((2, arcs // ROW)),
            dma((7,)),
            dma((7,)),
        ],
        compiler_params=pltpu.CompilerParams(
            collective_id=0, has_side_effects=True, vmem_limit_bytes=63 * 1024 * 1024 - 65536
        ),
    )(
        prev_dist, source_node.reshape(1, rows), arc_tail, base_cost, arc_price, capacity,
        path_arcs, demand,
    )


def solution(mesh):
    in_specs = (
        P("comm", "arc"),
        P("comm"),
        P(None, "arc"),
        P(None, "arc"),
        P(None, "arc"),
        P(None, "arc"),
        P(("comm", "arc"), None),
        P(("comm", "arc")),
    )
    out_specs = (P("comm", "arc"), P(None, "arc"))
    return jax.shard_map(shards, mesh=mesh, in_specs=in_specs, out_specs=out_specs, check_vma=False)
```

time: 66 us -> 51.7 us (0.78)
  Pallas kernels: 58.5 us -> 49.7 us
  local copies, waits for them, and re-layouts: 6.37 us -> 1.26 us
    pallas_call x1, Pallas kernels: 58.5 us -> 49.7 us  [shards(): pl.pallas_call(functools.partial(kernel, arcs, comms, arcs * span), out_s...]
    unnamed x18 -> x2, local copies, waits for them, and re-layouts: 6.37 us -> 1.26 us
where the time goes in v2:
time: 51.7 us; the launch traced here: 51.6 us
  Pallas kernels  49.7 us (96%)
  local copies, waits for them, and re-layouts  1.26 us (2%)
  between operations  0.64 us (1%)
    pallas_call x1, Pallas kernels, shards(): pl.pallas_call(functools.partial(kernel, arcs, comms, arcs * span), out_s...  49.7 us
    unnamed x2, local copies, waits for them, and re-layouts  1.26 us

profile of v2, /device:TPU:32, one launch (start us, length us, event | category | flops | bytes accessed | tf_op | source)
XLA Modules:
  0.0 51.6 jit_solution(5060210456060224200)
XLA Ops:
  0.6 49.7 %shard_map.95 = (f32[128,256]{1,0:T(8,128)S(1)}, f32[16,256]{1,0:T(8,128)S(1)}) custom-call(f32[128,256]{1,0:T(8,128)} %dist_hbm.1, s32[1,128]{1,0:T(1,128)} %bitcast.1, s32[16,256]{1,0:T(8,128)} %tail_hbm.1, f32[16,256]{1,0:T(8,128)} %cost_hbm.1, f32[16,256]{1,0:T(8,128)} %price_hbm.1, f32[16,256]{1,0:T(8,128)} %cap_hbm.1, s32[4,128]{1,0:T(4,128)} %path_hbm.1, ...), custom_call_target="tpu_custom_call" | custom-call | tf_op jit(solution)/shard_map/pallas_call | solution.py:343
  50.3 0.7 %copy.12 = f32[128,256]{1,0:T(8,128)} copy(f32[128,256]{1,0:T(8,128)S(1)} %get-tuple-element.2) | data formatting | bytes 262144
  50.9 0.6 %copy.13 = f32[16,256]{1,0:T(8,128)} copy(f32[16,256]{1,0:T(8,128)S(1)} %get-tuple-element.3) | data formatting | bytes 32768

commit v3 on v2

--- a/solution.py
+++ b/solution.py
@@ -31,9 +31,9 @@
     dist_hbm, source_hbm, tail_hbm, cost_hbm, price_hbm, cap_hbm, path_hbm, demand_ref,
     dist_out, price_out,
     dist_ref, source_ref, tail_ref, cost_ref, price_ref, cap_ref, path_ref, fetch_sem,
-    own, left, right, best, lhs, hot, rel, weight,
+    own, reduced, beside, across, missing, best, lhs, hot, seen, rel, weight, tell, told,
     pay, routes, ends, picks, flow, flows, square, squares, square_sum, square_sums,
-    near_send, near_recv, row_send, row_recv, col_send, col_recv, flow_send, flow_recv,
+    near_send, near_recv, tell_send, tell_recv, row_send, row_recv, col_send, col_recv, flow_send, flow_recv,
 ):
     me = lax.axis_index("arc")
     group = lax.axis_index("comm")
@@ -61,6 +61,9 @@
     for fetch in fetches:
         fetch.start()
 
+    core = lax.rem(me, 2)
+    partner = me + 1 - 2 * core
+    other = lax.rem(me + arcs - 1 + 2 * core, arcs)
     line = me // ROW
     place = lax.rem(me, ROW)
     lines = arcs // ROW
@@ -107,40 +110,65 @@
         rel[h] = pair
         at = pair // LANES
         inside = (at == 2) | (at == 3)
-        near = (at == 1) | (at == 4)
+        low = at < 2
+        toward = jnp.where(low, core, 1 - core) == 1
         weight[0, h] = jnp.where(inside, cost, jnp.inf)
-        weight[1, h] = jnp.where(near, cost, jnp.inf)
-        weight[2, h] = jnp.where(inside | near, jnp.inf, cost)
+        weight[1, h] = jnp.where(inside | ~toward, jnp.inf, cost)
+        weight[2, h] = jnp.where(inside | toward, jnp.inf, cost)
+        tell[0, h] = pair.astype(F32)
+        tell[1, h] = weight[2, h]
 
     row = lax.broadcasted_iota(jnp.int32, (LANES, span), 0)
+
+    def fill(target, h, t, k, want, at):
+        one = jnp.where(want - at * LANES == row, F32(1.0), F32(0.0)).astype(HOT)
+        target[h, t, k * span : k * span + LANES, :] = one
+        target[h, t, k * span + LANES : (k + 1) * span, :] = one
 
     @pl.loop(0, 8)
     def _(t):
         for h in range(2):
             want = jnp.broadcast_to(rel[h, pl.ds(t, 1), :], (LANES, span))
-            for k, at in enumerate((2, 3, 1, 4, 0 if h == 0 else 5)):
-                one = jnp.where(want == row + at * LANES, F32(1.0), F32(0.0)).astype(HOT)
-                hot[h, t, k * span : k * span + LANES, :] = one
-                hot[h, t, k * span + LANES : (k + 1) * span, :] = one
+            for k, at in enumerate(
+                (2, 3, 4 * (1 - core), 4 * (1 - core) + 1, 4 * core, 4 * core + 1)
+            ):
+                fill(hot, h, t, k, want, at)
+
+    for k in range(2):
+        for c in range(CHUNKS):
+            for b in range(2):
+                missing[k, c, b] = jnp.full((rows, LANES), jnp.inf, F32)
 
     pl.semaphore_wait(barrier, len(greeted))
 
-    def near_copies(slot, c):
-        out = []
-        for k, (b, there, target) in enumerate(
-            ((1, left, after), (0, right, before), (0, left, after), (1, right, before))
-        ):
-            out.append(
-                pltpu.make_async_remote_copy(
-                    src_ref=own.at[slot, c, b],
-                    dst_ref=there.at[slot, c, b],
-                    send_sem=near_send.at[slot, c, k],
-                    recv_sem=near_recv.at[slot, c, k],
-                    device_id={"arc": target},
-                    device_id_type=MESH,
-                )
-            )
-        return out
+    def to_partner(sweep, c):
+        return pltpu.make_async_remote_copy(
+            src_ref=own.at[sweep, c],
+            dst_ref=beside.at[sweep, c],
+            send_sem=near_send.at[0, sweep, c],
+            recv_sem=near_recv.at[0, sweep, c],
+            device_id={"arc": partner},
+            device_id_type=MESH,
+        )
+
+    def to_other(sweep, c, source_at):
+        return pltpu.make_async_remote_copy(
+            src_ref=source_at,
+            dst_ref=across.at[sweep, c],
+            send_sem=near_send.at[1, sweep, c],
+            recv_sem=near_recv.at[1, sweep, c],
+            device_id={"arc": other},
+            device_id_type=MESH,
+        )
+
+    arcs_told = pltpu.make_async_remote_copy(
+        src_ref=tell,
+        dst_ref=told,
+        send_sem=tell_send,
+        recv_sem=tell_recv,
+        device_id={"arc": other},
+        device_id_type=MESH,
+    )
 
     def row_copies(kind, source_at, target_at):
         return [
@@ -199,14 +227,35 @@
         for copy in copies:
             copy.wait_recv()
 
-    def phase(p, c, h, start, width, best_dist):
-        cols = slice(start, start + width)
-        taken = slice((0, 512, 1024)[p], (0, 512, 1024)[p] + width)
+    def phase(p, c, h, best_dist):
         for t in range(8):
-            found = jnp.dot(lhs[c, :, cols], hot[h, t, taken, :], preferred_element_type=F32)
+            found = jnp.dot(
+                lhs[c, :, p * 512 : (p + 1) * 512],
+                hot[h, t, p * 512 : (p + 1) * 512, :],
+                preferred_element_type=F32,
+            )
             found = found + weight[p, h, t : t + 1, :]
             best_dist = jnp.minimum(best_dist, jnp.minimum(found[:, :LANES], found[:, LANES:]))
         return best_dist
+
+    def given(c, h):
+        best_dist = jnp.full((rows, LANES), jnp.inf, F32)
+        for t in range(8):
+            found = jnp.dot(lhs[c, :, :512], seen[h, t], preferred_element_type=F32)
+            found = found + told[1, h, t : t + 1, :]
+            best_dist = jnp.minimum(best_dist, jnp.minimum(found[:, :LANES], found[:, LANES:]))
+        return best_dist
+
+    def learn():
+        arcs_told.wait_recv()
+
+        @pl.loop(0, 8)
+        def _(t):
+            for h in range(2):
+                want = told[0, h, pl.ds(t, 1), :].astype(jnp.int32)
+                want = jnp.broadcast_to(want, (LANES, span))
+                for k in range(2):
+                    fill(seen, h, t, k, want, 4 * (1 - core) + k)
 
     def put(c, place, block):
         high, low = parts(block)
@@ -284,53 +333,59 @@
                 price_ref[...] + F32(step_size) * flow[...] / root, F32(0.0)
             )
 
-    def send(slot, c):
-        start(near_copies(slot, c))
-
-    def inner(slot, c):
-        for b in range(2):
-            put(c, b, own[slot, c, b])
-        for h in range(2):
-            best[c, h] = phase(0, c, h, 0, 512, own[slot, c, h])
-
-    def outer(slot, c):
-        copies = near_copies(slot, c)
-        copies[0].wait_recv()
-        copies[1].wait_recv()
-        put(c, 2, left[slot, c, 1])
-        put(c, 3, right[slot, c, 0])
-        for h in range(2):
-            best[c, h] = phase(1, c, h, 512, 512, best[c, h])
-        copies[2].wait_recv()
-        copies[3].wait_recv()
-        put(c, 4, left[slot, c, 0])
-        put(c, 5, right[slot, c, 1])
-        for copy in copies:
-            copy.wait_send()
-        for h in range(2):
-            own[1 - slot, c, h] = phase(2, c, h, 1024 + h * span, span, best[c, h])
-
     for c in range(CHUNKS):
-        send(0, c)
+        to_other(0, c, own.at[0, c]).start()
+        to_partner(0, c).start()
+    arcs_told.start()
     start(row_pay)
 
     @pl.loop(0, SWEEPS)
     def _(sweep):
         slot = lax.rem(sweep, 2)
         for c in range(CHUNKS):
-            inner(slot, c)
+            for b in range(2):
+                put(c, b, own[sweep, c, b])
+            for h in range(2):
+                best[c, h] = phase(0, c, h, own[sweep, c, h])
+        for c in range(CHUNKS):
+            to_partner(sweep, c).wait_recv()
+            for b in range(2):
+                put(c, 2 + b, beside[sweep, c, b])
+            for h in range(2):
+                reduced[sweep, c, h] = phase(1, c, h, best[c, h])
+
+            @pl.when(sweep < SWEEPS - 1)
+            def _():
+                to_other(sweep + 1, c, reduced.at[sweep, c]).start()
+
+        pl.when(sweep == 0)(learn)
+        for c in range(CHUNKS):
+            for h in range(2):
+                missing[slot, c, h] = given(c, h)
         for t in range(SWEEPS):
             pl.when(sweep == t)(functools.partial(flow_step, t))
         for c in range(CHUNKS):
-            outer(slot, c)
+            to_other(sweep, c, own.at[0, c]).wait_recv()
+            for b in range(2):
+                put(c, 4 + b, jnp.minimum(across[sweep, c, b], missing[1 - slot, c, b]))
+            for h in range(2):
+                own[sweep + 1, c, h] = phase(2, c, h, reduced[sweep, c, h])
 
             @pl.when(sweep < SWEEPS - 1)
             def _():
-                send(1 - slot, c)
+                to_partner(sweep + 1, c).start()
 
     for c in range(CHUNKS):
         for b in range(2):
-            dist_out[c * rows : (c + 1) * rows, b * LANES : (b + 1) * LANES] = own[SWEEPS % 2, c, b]
+            dist_out[c * rows : (c + 1) * rows, b * LANES : (b + 1) * LANES] = own[SWEEPS, c, b]
+
+    arcs_told.wait_send()
+
+    @pl.loop(0, SWEEPS)
+    def _(sweep):
+        for c in range(CHUNKS):
+            to_partner(sweep, c).wait_send()
+            to_other(sweep, c, own.at[0, c]).wait_send()
 
 
 def shards(prev_dist, source_node, arc_tail, base_cost, arc_price, capacity, path_arcs, demand):
@@ -357,14 +412,19 @@
             pltpu.VMEM(arc_price.shape, F32),
             pltpu.VMEM(path_arcs.shape, jnp.int32),
             dma((7,)),
-            pltpu.VMEM((2, CHUNKS, 2, rows // CHUNKS, LANES), F32),
-            pltpu.VMEM((2, CHUNKS, 2, rows // CHUNKS, LANES), F32),
+            pltpu.VMEM((SWEEPS + 1, CHUNKS, 2, rows // CHUNKS, LANES), F32),
+            pltpu.VMEM((SWEEPS, CHUNKS, 2, rows // CHUNKS, LANES), F32),
+            pltpu.VMEM((SWEEPS, CHUNKS, 2, rows // CHUNKS, LANES), F32),
+            pltpu.VMEM((SWEEPS, CHUNKS, 2, rows // CHUNKS, LANES), F32),
             pltpu.VMEM((2, CHUNKS, 2, rows // CHUNKS, LANES), F32),
             pltpu.VMEM((CHUNKS, 2, rows // CHUNKS, LANES), F32),
             pltpu.VMEM((CHUNKS, rows // CHUNKS, 12 * LANES), BF16),
-            pltpu.VMEM((2, 8, 10 * LANES, span), HOT),
+            pltpu.VMEM((2, 8, 12 * LANES, span), HOT),
+            pltpu.VMEM((2, 8, 4 * LANES, span), HOT),
             pltpu.VMEM((2, 8, span), jnp.int32),
             pltpu.VMEM((3, 2, 8, span), F32),
+            pltpu.VMEM((2, 2, 8, span), F32),
+            pltpu.VMEM((2, 2, 8, span), F32),
             pltpu.VMEM((8, LANES), F32),
             pltpu.VMEM((arcs, 8, LANES), F32),
             pltpu.VMEM((span, 32 * LANES), BF16),
@@ -375,8 +435,10 @@
             pltpu.VMEM((ROW, 8, LANES), F32),
             pltpu.VMEM((8, LANES), F32),
             pltpu.VMEM((arcs // ROW, 8, LANES), F32),
-            dma((2, CHUNKS, 4)),
-            dma((2, CHUNKS, 4)),
+            dma((2, SWEEPS, CHUNKS)),
+            dma((2, SWEEPS, CHUNKS)),
+            dma,
+            dma,
             dma((2, ROW)),
             dma((2, ROW)),
             dma((2, arcs // ROW)),

time: 51.7 us -> 50.2 us (0.971)
  the two profiles are of different devices: /device:TPU:32 before, /device:TPU:1 now
where the time goes in v3:
time: 50.2 us; the launch traced here: 50 us
  Pallas kernels  48.1 us (96%)
  local copies, waits for them, and re-layouts  1.26 us (3%)
  between operations  0.64 us (1%)
    pallas_call x1, Pallas kernels, shards(): pl.pallas_call(functools.partial(kernel, arcs, comms, arcs * span), out_s...  48.1 us
    unnamed x2, local copies, waits for them, and re-layouts  1.26 us

profile of v3, /device:TPU:1, one launch (start us, length us, event | category | flops | bytes accessed | tf_op | source)
XLA Modules:
  0.0 50.0 jit_solution(15615440900024808219)
XLA Ops:
  0.6 48.1 %shard_map.95 = (f32[128,256]{1,0:T(8,128)S(1)}, f32[16,256]{1,0:T(8,128)S(1)}) custom-call(f32[128,256]{1,0:T(8,128)} %dist_hbm.1, s32[1,128]{1,0:T(1,128)} %bitcast.1, s32[16,256]{1,0:T(8,128)} %tail_hbm.1, f32[16,256]{1,0:T(8,128)} %cost_hbm.1, f32[16,256]{1,0:T(8,128)} %price_hbm.1, f32[16,256]{1,0:T(8,128)} %cap_hbm.1, s32[4,128]{1,0:T(4,128)} %path_hbm.1, ...), custom_call_target="tpu_custom_call" | custom-call | tf_op jit(solution)/shard_map/pallas_call | solution.py:398
  48.8 0.7 %copy.12 = f32[128,256]{1,0:T(8,128)} copy(f32[128,256]{1,0:T(8,128)S(1)} %get-tuple-element.2) | data formatting | bytes 262144
  49.4 0.6 %copy.13 = f32[16,256]{1,0:T(8,128)} copy(f32[16,256]{1,0:T(8,128)S(1)} %get-tuple-element.3) | data formatting | bytes 32768

commit v4 on v3

--- a/solution.py
+++ b/solution.py
@@ -8,7 +8,7 @@
 from jax.sharding import PartitionSpec as P
 
 SWEEPS = 8
-CHUNKS = 2
+CHUNKS = 1
 
 LANES = 128
 MESH = pl.DeviceIdType.MESH
@@ -130,7 +130,14 @@
         for h in range(2):
             want = jnp.broadcast_to(rel[h, pl.ds(t, 1), :], (LANES, span))
             for k, at in enumerate(
-                (2, 3, 4 * (1 - core), 4 * (1 - core) + 1, 4 * core, 4 * core + 1)
+                (
+                    2 + core,
+                    3 - core,
+                    4 * (1 - core) + core,
+                    4 * (1 - core) + 1 - core,
+                    4 * core + 1 - core,
+                    4 * core + core,
+                )
             ):
                 fill(hot, h, t, k, want, at)
 
@@ -227,24 +234,31 @@
         for copy in copies:
             copy.wait_recv()
 
-    def phase(p, c, h, best_dist):
+    def least(c, start, width, table, costs, best_dist):
         for t in range(8):
             found = jnp.dot(
-                lhs[c, :, p * 512 : (p + 1) * 512],
-                hot[h, t, p * 512 : (p + 1) * 512, :],
-                preferred_element_type=F32,
-            )
-            found = found + weight[p, h, t : t + 1, :]
+                lhs[c, :, start : start + width], table(t), preferred_element_type=F32
+            )
+            found = found + costs(t)
             best_dist = jnp.minimum(best_dist, jnp.minimum(found[:, :LANES], found[:, LANES:]))
         return best_dist
 
-    def given(c, h):
-        best_dist = jnp.full((rows, LANES), jnp.inf, F32)
-        for t in range(8):
-            found = jnp.dot(lhs[c, :, :512], seen[h, t], preferred_element_type=F32)
-            found = found + told[1, h, t : t + 1, :]
-            best_dist = jnp.minimum(best_dist, jnp.minimum(found[:, :LANES], found[:, LANES:]))
-        return best_dist
+    def phase(p, c, h, width, best_dist):
+        start = p * 512
+        return least(
+            c, start, width,
+            lambda t: hot[h, t, start : start + width, :],
+            lambda t: weight[p, h, t : t + 1, :],
+            best_dist,
+        )
+
+    def given(c, h, width):
+        return least(
+            c, 0, width,
+            lambda t: seen[h, t, :width, :],
+            lambda t: told[1, h, t : t + 1, :],
+            jnp.full((rows, LANES), jnp.inf, F32),
+        )
 
     def learn():
         arcs_told.wait_recv()
@@ -255,7 +269,8 @@
                 want = told[0, h, pl.ds(t, 1), :].astype(jnp.int32)
                 want = jnp.broadcast_to(want, (LANES, span))
                 for k in range(2):
-                    fill(seen, h, t, k, want, 4 * (1 - core) + k)
+                    at = 4 * (1 - core) + (core if k == 0 else 1 - core)
+                    fill(seen, h, t, k, want, at)
 
     def put(c, place, block):
         high, low = parts(block)
@@ -273,7 +288,7 @@
                 amount = routes[base + i, 4 + r : 5 + r, :]
                 node = jnp.broadcast_to((ids & (nodes - 1)) - first, (span, LANES))
                 hop_slot = jnp.broadcast_to(ids // nodes, (16, LANES))
-                ends[:, at] = jnp.where(node == node_row, F32(1.0), F32(0.0)).astype(BF16)
+                ends[:, at] = jnp.where(node == node_row, F32(1.0), F32(0.0)).astype(HOT)
                 given = jnp.where(hop_slot == slot_row, amount, F32(0.0))
                 high, low = parts(given)
                 picks[0:16, at] = high
@@ -343,33 +358,43 @@
     def _(sweep):
         slot = lax.rem(sweep, 2)
         for c in range(CHUNKS):
-            for b in range(2):
-                put(c, b, own[sweep, c, b])
+            for k, b in enumerate((core, 1 - core)):
+                put(c, k, own[sweep, c, b])
             for h in range(2):
-                best[c, h] = phase(0, c, h, own[sweep, c, h])
+                best[c, h] = phase(0, c, h, 512, own[sweep, c, h])
+
+        @pl.when(sweep > 0)
+        def _():
+            for c in range(CHUNKS):
+                for h, width in ((1 - core, 512), (core, 256)):
+                    missing[slot, c, h] = given(c, h, width)
+
         for c in range(CHUNKS):
             to_partner(sweep, c).wait_recv()
-            for b in range(2):
-                put(c, 2 + b, beside[sweep, c, b])
-            for h in range(2):
-                reduced[sweep, c, h] = phase(1, c, h, best[c, h])
+            for k, b in enumerate((core, 1 - core)):
+                put(c, 2 + k, beside[sweep, c, b])
+            for h, width in ((1 - core, 512), (core, 256)):
+                reduced[sweep, c, h] = phase(1, c, h, width, best[c, h])
 
             @pl.when(sweep < SWEEPS - 1)
             def _():
                 to_other(sweep + 1, c, reduced.at[sweep, c]).start()
 
-        pl.when(sweep == 0)(learn)
-        for c in range(CHUNKS):
-            for h in range(2):
-                missing[slot, c, h] = given(c, h)
+        @pl.when(sweep == 0)
+        def _():
+            learn()
+            for c in range(CHUNKS):
+                for h, width in ((1 - core, 512), (core, 256)):
+                    missing[slot, c, h] = given(c, h, width)
+
         for t in range(SWEEPS):
             pl.when(sweep == t)(functools.partial(flow_step, t))
         for c in range(CHUNKS):
             to_other(sweep, c, own.at[0, c]).wait_recv()
-            for b in range(2):
-                put(c, 4 + b, jnp.minimum(across[sweep, c, b], missing[1 - slot, c, b]))
-            for h in range(2):
-                own[sweep + 1, c, h] = phase(2, c, h, reduced[sweep, c, h])
+            for k, b in enumerate((1 - core, core)):
+                put(c, 4 + k, jnp.minimum(across[sweep, c, b], missing[1 - slot, c, b]))
+            for h, width in ((core, 512), (1 - core, 256)):
+                own[sweep + 1, c, h] = phase(2, c, h, width, reduced[sweep, c, h])
 
             @pl.when(sweep < SWEEPS - 1)
             def _():
@@ -427,7 +452,7 @@
             pltpu.VMEM((2, 2, 8, span), F32),
             pltpu.VMEM((8, LANES), F32),
             pltpu.VMEM((arcs, 8, LANES), F32),
-            pltpu.VMEM((span, 32 * LANES), BF16),
+            pltpu.VMEM((span, 32 * LANES), HOT),
             pltpu.VMEM((32, 32 * LANES), BF16),
             pltpu.VMEM((16, span), F32),
             pltpu.VMEM((comms, 16, span), F32),

time: 50.2 us -> 45.7 us (0.910)
  Pallas kernels: 48.1 us -> 43.7 us
    pallas_call x1, Pallas kernels: 48.1 us -> 43.7 us  [shards(): pl.pallas_call(functools.partial(kernel, arcs, comms, arcs * span), out_s...]
where the time goes in v4:
time: 45.7 us; the launch traced here: 45.6 us
  Pallas kernels  43.7 us (96%)
  local copies, waits for them, and re-layouts  1.26 us (3%)
  between operations  0.64 us (1%)
    pallas_call x1, Pallas kernels, shards(): pl.pallas_call(functools.partial(kernel, arcs, comms, arcs * span), out_s...  43.7 us
    unnamed x2, local copies, waits for them, and re-layouts  1.26 us

profile of v4, /device:TPU:1, one launch (start us, length us, event | category | flops | bytes accessed | tf_op | source)
XLA Modules:
  0.0 45.6 jit_solution(15989232665934302500)
XLA Ops:
  0.6 43.7 %shard_map.95 = (f32[128,256]{1,0:T(8,128)S(1)}, f32[16,256]{1,0:T(8,128)S(1)}) custom-call(f32[128,256]{1,0:T(8,128)} %dist_hbm.1, s32[1,128]{1,0:T(1,128)} %bitcast.1, s32[16,256]{1,0:T(8,128)} %tail_hbm.1, f32[16,256]{1,0:T(8,128)} %cost_hbm.1, f32[16,256]{1,0:T(8,128)} %price_hbm.1, f32[16,256]{1,0:T(8,128)} %cap_hbm.1, s32[4,128]{1,0:T(4,128)} %path_hbm.1, ...), custom_call_target="tpu_custom_call" | custom-call | tf_op jit(solution)/shard_map/pallas_call | solution.py:423
  44.3 0.7 %copy.12 = f32[128,256]{1,0:T(8,128)} copy(f32[128,256]{1,0:T(8,128)S(1)} %get-tuple-element.2) | data formatting | bytes 262144
  45.0 0.6 %copy.13 = f32[16,256]{1,0:T(8,128)} copy(f32[16,256]{1,0:T(8,128)S(1)} %get-tuple-element.3) | data formatting | bytes 32768

commit v5 on v4

--- a/solution.py
+++ b/solution.py
@@ -125,27 +125,6 @@
         target[h, t, k * span : k * span + LANES, :] = one
         target[h, t, k * span + LANES : (k + 1) * span, :] = one
 
-    @pl.loop(0, 8)
-    def _(t):
-        for h in range(2):
-            want = jnp.broadcast_to(rel[h, pl.ds(t, 1), :], (LANES, span))
-            for k, at in enumerate(
-                (
-                    2 + core,
-                    3 - core,
-                    4 * (1 - core) + core,
-                    4 * (1 - core) + 1 - core,
-                    4 * core + 1 - core,
-                    4 * core + core,
-                )
-            ):
-                fill(hot, h, t, k, want, at)
-
-    for k in range(2):
-        for c in range(CHUNKS):
-            for b in range(2):
-                missing[k, c, b] = jnp.full((rows, LANES), jnp.inf, F32)
-
     pl.semaphore_wait(barrier, len(greeted))
 
     def to_partner(sweep, c):
@@ -278,44 +257,47 @@
         lhs[c, :, place * span + LANES : (place + 1) * span] = low
 
     def count_line(step):
-        node_row = lax.broadcasted_iota(jnp.int32, (span, LANES), 0)
-        slot_row = lax.broadcasted_iota(jnp.int32, (16, LANES), 0)
+        node_row = lax.broadcasted_iota(jnp.int32, (LANES, LANES), 0)
+        place_row = lax.broadcasted_iota(jnp.int32, (32, LANES), 0)
         base = lax.rem(line + step, lines) * ROW
         for i in range(ROW):
             for r in range(4):
                 at = slice((i * 4 + r) * LANES, (i * 4 + r + 1) * LANES)
                 ids = routes[base + i, r : r + 1, :].astype(jnp.int32)
                 amount = routes[base + i, 4 + r : 5 + r, :]
-                node = jnp.broadcast_to((ids & (nodes - 1)) - first, (span, LANES))
-                hop_slot = jnp.broadcast_to(ids // nodes, (16, LANES))
-                ends[:, at] = jnp.where(node == node_row, F32(1.0), F32(0.0)).astype(HOT)
-                given = jnp.where(hop_slot == slot_row, amount, F32(0.0))
-                high, low = parts(given)
-                picks[0:16, at] = high
-                picks[16:32, at] = low
+                node = (ids & (nodes - 1)) - first
+                here = (node >= 0) & (node < span)
+                spot = jnp.where(here, (node // LANES) * 16 + ids // nodes, -1)
+                lane_of = jnp.broadcast_to(node & (LANES - 1), (LANES, LANES))
+                ends[:, at] = jnp.where(lane_of == node_row, F32(1.0), F32(0.0)).astype(HOT)
+                carried = jnp.where(
+                    jnp.broadcast_to(spot, (32, LANES)) == place_row, amount, F32(0.0)
+                )
+                high, low = parts(carried)
+                picks[0:32, at] = high
+                picks[32:64, at] = low
         both = lax.dot_general(
             picks[...], ends[...], (((1,), (1,)), ((), ())), preferred_element_type=F32
         )
-        return both[0:16] + both[16:32]
+        both = both[0:32] + both[32:64]
+        return jnp.concatenate([both[0:16], both[16:32]], axis=1)
 
     def flow_step(t):
         if t == 0:
             finish(row_pay)
             routes[me] = pay[...]
             start(col_pay)
+            flow[...] = count_line(0)
         if t == 1:
-            flow[...] = count_line(0)
-        if t == 2:
             finish(col_pay)
 
-            @pl.loop(1, 3)
+            @pl.loop(1, lines)
             def _(step):
                 flow[...] += count_line(step)
-        if t == 3:
-            flow[...] += count_line(3)
+
             flows[group] = flow[...]
             start(near_flow)
-        if t == 4:
+        if t == 3:
             finish(near_flow)
             start(far_flow)
         if t == 5:
@@ -354,6 +336,27 @@
     arcs_told.start()
     start(row_pay)
 
+    @pl.loop(0, 8)
+    def _(t):
+        for h in range(2):
+            want = jnp.broadcast_to(rel[h, pl.ds(t, 1), :], (LANES, span))
+            for k, at in enumerate(
+                (
+                    2 + core,
+                    3 - core,
+                    4 * (1 - core) + core,
+                    4 * (1 - core) + 1 - core,
+                    4 * core + 1 - core,
+                    4 * core + core,
+                )
+            ):
+                fill(hot, h, t, k, want, at)
+
+    for k in range(2):
+        for c in range(CHUNKS):
+            for b in range(2):
+                missing[k, c, b] = jnp.full((rows, LANES), jnp.inf, F32)
+
     @pl.loop(0, SWEEPS)
     def _(sweep):
         slot = lax.rem(sweep, 2)
@@ -363,7 +366,7 @@
             for h in range(2):
                 best[c, h] = phase(0, c, h, 512, own[sweep, c, h])
 
-        @pl.when(sweep > 0)
+        @pl.when((sweep > 0) & (sweep < SWEEPS - 1))
         def _():
             for c in range(CHUNKS):
                 for h, width in ((1 - core, 512), (core, 256)):
@@ -452,8 +455,8 @@
             pltpu.VMEM((2, 2, 8, span), F32),
             pltpu.VMEM((8, LANES), F32),
             pltpu.VMEM((arcs, 8, LANES), F32),
-            pltpu.VMEM((span, 32 * LANES), HOT),
-            pltpu.VMEM((32, 32 * LANES), BF16),
+            pltpu.VMEM((LANES, 32 * LANES), HOT),
+            pltpu.VMEM((64, 32 * LANES), BF16),
             pltpu.VMEM((16, span), F32),
             pltpu.VMEM((comms, 16, span), F32),
             pltpu.VMEM((8, LANES), F32),

time: 45.7 us -> 47.3 us (1.035)
  Pallas kernels: 43.7 us -> 45.2 us
    pallas_call x1, Pallas kernels: 43.7 us -> 45.2 us  [shards(): pl.pallas_call(functools.partial(kernel, arcs, comms, arcs * span), out_s...]
where the time goes in v5:
time: 47.3 us; the launch traced here: 47.1 us
  Pallas kernels  45.2 us (96%)
  local copies, waits for them, and re-layouts  1.26 us (3%)
  between operations  0.64 us (1%)
    pallas_call x1, Pallas kernels, shards(): pl.pallas_call(functools.partial(kernel, arcs, comms, arcs * span), out_s...  45.2 us
    unnamed x2, local copies, waits for them, and re-layouts  1.26 us

profile of v5, /device:TPU:1, one launch (start us, length us, event | category | flops | bytes accessed | tf_op | source)
XLA Modules:
  0.0 47.1 jit_solution(7120215071031766831)
XLA Ops:
  0.6 45.2 %shard_map.95 = (f32[128,256]{1,0:T(8,128)S(1)}, f32[16,256]{1,0:T(8,128)S(1)}) custom-call(f32[128,256]{1,0:T(8,128)} %dist_hbm.1, s32[1,128]{1,0:T(1,128)} %bitcast.1, s32[16,256]{1,0:T(8,128)} %tail_hbm.1, f32[16,256]{1,0:T(8,128)} %cost_hbm.1, f32[16,256]{1,0:T(8,128)} %price_hbm.1, f32[16,256]{1,0:T(8,128)} %cap_hbm.1, s32[4,128]{1,0:T(4,128)} %path_hbm.1, ...), custom_call_target="tpu_custom_call" | custom-call | tf_op jit(solution)/shard_map/pallas_call | solution.py:426
  45.9 0.7 %copy.12 = f32[128,256]{1,0:T(8,128)} copy(f32[128,256]{1,0:T(8,128)S(1)} %get-tuple-element.2) | data formatting | bytes 262144
  46.5 0.6 %copy.13 = f32[16,256]{1,0:T(8,128)} copy(f32[16,256]{1,0:T(8,128)S(1)} %get-tuple-element.3) | data formatting | bytes 32768

commit v6 on v5

--- a/solution.py
+++ b/solution.py
@@ -290,14 +290,12 @@
             flow[...] = count_line(0)
         if t == 1:
             finish(col_pay)
-
-            @pl.loop(1, lines)
-            def _(step):
-                flow[...] += count_line(step)
-
+        if t in (1, 2, 3):
+            flow[...] += count_line(t)
+        if t == 3:
             flows[group] = flow[...]
             start(near_flow)
-        if t == 3:
+        if t == 4:
             finish(near_flow)
             start(far_flow)
         if t == 5:

time: 47.3 us -> 46.7 us (0.987)
  Pallas kernels: 45.2 us -> 44.6 us
    pallas_call x1, Pallas kernels: 45.2 us -> 44.6 us  [shards(): pl.pallas_call(functools.partial(kernel, arcs, comms, arcs * span), out_s...]
where the time goes in v6:
time: 46.7 us; the launch traced here: 46.6 us
  Pallas kernels  44.6 us (96%)
  local copies, waits for them, and re-layouts  1.26 us (3%)
  between operations  0.64 us (1%)
    pallas_call x1, Pallas kernels, shards(): pl.pallas_call(functools.partial(kernel, arcs, comms, arcs * span), out_s...  44.6 us
    unnamed x2, local copies, waits for them, and re-layouts  1.26 us

profile of v6, /device:TPU:1, one launch (start us, length us, event | category | flops | bytes accessed | tf_op | source)
XLA Modules:
  0.0 46.6 jit_solution(8845012486994859505)
XLA Ops:
  0.6 44.6 %shard_map.95 = (f32[128,256]{1,0:T(8,128)S(1)}, f32[16,256]{1,0:T(8,128)S(1)}) custom-call(f32[128,256]{1,0:T(8,128)} %dist_hbm.1, s32[1,128]{1,0:T(1,128)} %bitcast.1, s32[16,256]{1,0:T(8,128)} %tail_hbm.1, f32[16,256]{1,0:T(8,128)} %cost_hbm.1, f32[16,256]{1,0:T(8,128)} %price_hbm.1, f32[16,256]{1,0:T(8,128)} %cap_hbm.1, s32[4,128]{1,0:T(4,128)} %path_hbm.1, ...), custom_call_target="tpu_custom_call" | custom-call | tf_op jit(solution)/shard_map/pallas_call | solution.py:424
  45.3 0.7 %copy.12 = f32[128,256]{1,0:T(8,128)} copy(f32[128,256]{1,0:T(8,128)S(1)} %get-tuple-element.2) | data formatting | bytes 262144
  45.9 0.6 %copy.13 = f32[16,256]{1,0:T(8,128)} copy(f32[16,256]{1,0:T(8,128)S(1)} %get-tuple-element.3) | data formatting | bytes 32768
